TPU v7x, 32 devices: a whole 2x2x4 slice. The times are simulated.
32 devices in a mesh: chain: 4 (over z), inner: 8 (over y, x, core).
Axes of the slice: x: 2, y: 2, z: 4, core: 2. Of those that a mesh axis runs over, the one named last changes fastest.
Arguments:
- queries: bfloat16 [4096, 4096], P(('chain', 'inner')), may hold values from -0.75 to 0.75
- key_rows: bfloat16 [4096, 4096], P(('chain', 'inner')), may hold values from -0.75 to 0.75
- value_rows: bfloat16 [4096, 4096], P(('chain', 'inner')), may hold values from -0.75 to 0.75
- out_grad: bfloat16 [4096, 4096], P(('chain', 'inner')), may hold values from -0.75 to 0.75
- log_decay: bfloat16 [4096, 32], P(('chain', 'inner')), may hold values from -2 to 0, as said below
Outputs:
- attended: bfloat16 [4096, 4096], P(('chain', 'inner'))
- query_grad: bfloat16 [4096, 4096], P(('chain', 'inner'))
- key_grad: bfloat16 [4096, 4096], P(('chain', 'inner'))
- value_grad: bfloat16 [4096, 4096], P(('chain', 'inner'))
Inputs may be any that keep to these rules, and one draw needn't show every extreme that they name: `log_decay`: every entry is negative.
All inputs are finite; a program needn't handle non-finite values.
Results may differ from a plain program's by a relative error of at most 0.0051.
Values may be sent and summed in bfloat16 or wider, within the bound.
A program may use at most 64 MiB of HBM per device.

v0:
```python
import functools

import jax
import jax.numpy as jnp
from jax import lax
from jax.experimental import pallas as pl
from jax.experimental.pallas import tpu as pltpu
from jax.sharding import PartitionSpec as P

SIZE = 128
F32 = jnp.float32
BF16 = jnp.bfloat16
MESH = pl.DeviceIdType.MESH


def triangle(rows):
    row = lax.broadcasted_iota(jnp.int32, (rows, rows), 0)
    column = lax.broadcasted_iota(jnp.int32, (rows, rows), 1)
    return row >= column


def spread_columns(decay, head, count):
    rows, heads = decay.shape
    row = lax.broadcasted_iota(jnp.int32, (heads, count * SIZE), 0)
    column = lax.broadcasted_iota(jnp.int32, (heads, count * SIZE), 1)
    begin = (row - head) * SIZE
    pick = ((column >= begin) & (column < begin + SIZE)).astype(F32).astype(BF16)
    spread = jnp.dot(decay, pick, preferred_element_type=F32).astype(BF16)
    lower = triangle(rows).astype(F32).astype(BF16)
    return jnp.dot(lower, spread, preferred_element_type=F32)


def over_rows(left, right):
    return lax.dot_general(left, right, (((0,), (0,)), ((), ())), preferred_element_type=F32)


def over_columns(left, right):
    return lax.dot_general(left, right, (((1,), (1,)), ((), ())), preferred_element_type=F32)


def states_kernel(
    planes, devices, q_any, k_any, v_any, g_any, decay_ref, states_ref,
    q_ref, k_ref, v_ref, g_ref, cumuls, local,
    cumul_rows, terms, from_core, to_chips, from_chips, plane_sum, from_planes, to_back, from_back, to_core,
    own_fin, core_fin, chip_fin, plane_fin,
    load_s, fin_s, fin_r, chip_fs, chip_fr, plane_fs, plane_fr,
    core_s, core_r, out_s, out_r, plane_s, plane_r, back_s, back_r, last_s, last_r,
):
    rows, heads = decay_ref.shape
    chips = devices // 2
    own = heads // devices
    z = lax.axis_index("chain")
    me = lax.axis_index("inner")
    chip, core = me // 2, lax.rem(me, 2)
    first_core = core == 0

    def at_core():
        return (z, chip * 2 + 1 - core)

    def at_chip(other):
        return (z, other * 2 + core)

    def at_plane(other):
        return (other, me)

    def remote(src, dst, send, recv, to):
        return pltpu.make_async_remote_copy(
            src_ref=src, dst_ref=dst, send_sem=send, recv_sem=recv, device_id=to, device_id_type=MESH
        )

    def loads(group, part):
        begin, width = (0, SIZE) if part == 0 else (SIZE, (own - 1) * SIZE)
        columns = pl.ds(pl.multiple_of(group * (own * SIZE) + begin, SIZE), width)
        pairs = ((q_any, q_ref), (k_any, k_ref), (v_any, v_ref), (g_any, g_ref))
        return [
            pltpu.make_async_copy(src.at[:, columns], dst.at[:, columns], load_s.at[j, group, part])
            for j, (src, dst) in enumerate(pairs)
        ]

    def owner(step, side):
        return lax.rem(chip + 1 + step, chips) * 2 + side

    for side in (1 - core, core):
        @pl.loop(0, chips)
        def _(step):
            for copy in loads(owner(step, side), 0):
                copy.start()

    if own > 1:
        for side in (1 - core, core):
            @pl.loop(0, chips)
            def _(step):
                for copy in loads(owner(step, side), 1):
                    copy.start()

    barrier = pltpu.get_barrier_semaphore()
    pl.semaphore_signal(barrier, inc=1, device_id=at_core(), device_id_type=MESH)
    for step in range(1, chips):
        pl.semaphore_signal(
            barrier, inc=1, device_id=at_chip(lax.rem(chip + step, chips)), device_id_type=MESH
        )
    for step in range(1, planes):
        pl.semaphore_signal(
            barrier, inc=1, device_id=at_plane(lax.rem(z + step, planes)), device_id_type=MESH
        )

    decay = decay_ref[...]
    own_fin[...] = over_rows(decay, jnp.ones((rows, SIZE), BF16))
    upper = jnp.logical_not(triangle(rows)) | (
        lax.broadcasted_iota(jnp.int32, (rows, rows), 0)
        == lax.broadcasted_iota(jnp.int32, (rows, rows), 1)
    )
    cumul_rows[...] = over_rows(decay, upper.astype(F32).astype(BF16))
    @pl.loop(0, heads // 4)
    def _(group):
        spread = spread_columns(decay, group * 4, 4)
        for j in range(4):
            cumuls[group * 4 + j] = spread[:, j * SIZE : (j + 1) * SIZE]

    from_planes[z] = jnp.zeros(from_planes.shape[1:], BF16)
    pl.semaphore_wait(barrier, chips + planes - 1)

    fin_copy = remote(own_fin, core_fin, fin_s, fin_r, at_core())
    fin_copy.start()

    def make_terms(head):
        cumul = cumuls[head]
        columns = pl.ds(pl.multiple_of(head * SIZE, SIZE), SIZE)
        final = cumul[rows - 1 :, :]
        keys = (k_ref[:, columns].astype(F32) * jnp.exp(final - cumul)).astype(BF16)
        queries = (q_ref[:, columns].astype(F32) * jnp.exp(cumul)).astype(BF16)
        terms[head, 0] = over_rows(keys, v_ref[:, columns])
        terms[head, 1] = over_rows(queries, g_ref[:, columns])

    def inside(head):
        columns = pl.ds(pl.multiple_of(head * SIZE, SIZE), SIZE)
        query, key, value, grad = (ref[:, columns] for ref in (q_ref, k_ref, v_ref, g_ref))
        spread = cumuls[head] - cumul_rows[pl.ds(head, 1), :]
        weights = jnp.exp(jnp.where(triangle(rows), spread, -jnp.inf))
        probs = (over_columns(query, key) * weights).astype(BF16)
        grows = (over_columns(grad, value) * weights).astype(BF16)
        local[0, head] = jnp.dot(probs, value, preferred_element_type=F32)
        local[1, head] = jnp.dot(grows, key, preferred_element_type=F32)
        local[2, head] = over_rows(grows, query)
        local[3, head] = over_rows(probs, grad)

    chunk = heads // 8

    def inside_chunk(at):
        @pl.loop(0, chunk // 2)
        def _(pair):
            for j in range(2):
                inside(at * chunk + pair * 2 + j)

    def core_copy(i, other):
        slot = other * own + i
        head = (other * 2 + 1 - core) * own + i
        return remote(
            terms.at[head], from_core.at[slot], core_s.at[slot], core_r.at[slot], at_core()
        )

    def wait_loads(step, side):
        for copy in loads(owner(step, side), 0):
            copy.wait()

    pairs = chips // 2

    def make(i, pair):
        steps = (pair * 2, pair * 2 + 1)

        @pl.when(i == 0)
        def _():
            for step in steps:
                wait_loads(step, 1 - core)
                wait_loads(step, core)

        if own > 1:
            @pl.when((i == 1) & (pair == 0))
            def _():
                @pl.loop(0, devices)
                def _(group):
                    for copy in loads(group, 1):
                        copy.wait()

        for side in (1 - core, core):
            for step in steps:
                make_terms(owner(step, side) * own + i)
        for step in steps:
            core_copy(i, lax.rem(chip + 1 + step, chips)).start()

    def out_copy(i, other):
        return remote(
            to_chips.at[other, i], from_chips.at[chip, i], out_s.at[other * own + i],
            out_r.at[chip * own + i], at_chip(other),
        )

    def out_arrival(i, other):
        return remote(
            to_chips.at[other, i], from_chips.at[other, i], out_s.at[other * own + i],
            out_r.at[other * own + i], at_chip(other),
        )

    def combine(i, step):
        other = lax.rem(chip + 1 + step, chips)
        core_copy(i, other).wait_recv()
        head = (other * 2 + core) * own + i
        slot = other * own + i
        mine = jnp.exp(own_fin[pl.ds(head, 1), :])
        theirs = jnp.exp(core_fin[pl.ds(head, 1), :])
        one = jnp.ones_like(mine)
        kv = (
            jnp.where(first_core, theirs, one) * terms[head, 0]
            + jnp.where(first_core, one, mine) * from_core[slot, 0]
        ).astype(BF16)
        qd = (
            jnp.where(first_core, one, theirs) * terms[head, 1]
            + jnp.where(first_core, mine, one) * from_core[slot, 1]
        ).astype(BF16)

        @pl.when(step < chips - 1)
        def _():
            to_chips[other, i, 0] = kv
            to_chips[other, i, 1] = qd
            out_copy(i, other).start()

        @pl.when(step == chips - 1)
        def _():
            from_chips[chip, i, 0] = kv
            from_chips[chip, i, 1] = qd

    make(0, 0)
    fin_copy.wait_recv()
    chip_fin[chip] = own_fin[...] + core_fin[...]

    def chip_fin_copy(other, slot):
        return remote(
            chip_fin.at[chip], chip_fin.at[slot], chip_fs.at[other], chip_fr.at[slot], at_chip(other)
        )

    for step in range(1, chips):
        chip_fin_copy(lax.rem(chip + step, chips), chip).start()

    def combine_pair(i, pair):
        for step in (pair * 2, pair * 2 + 1):
            combine(i, step)

    @pl.loop(1, own * pairs)
    def _(at):
        make(at // pairs, lax.rem(at, pairs))
        combine_pair((at - 1) // pairs, lax.rem(at - 1, pairs))

    combine_pair(own - 1, pairs - 1)

    for step in range(1, chips):
        other = lax.rem(chip + step, chips)
        chip_fin_copy(other, other).wait_recv()
    total = chip_fin[0]
    for other in range(1, chips):
        total = total + chip_fin[other]
    plane_fin[z] = total

    def plane_fin_copy(other, slot):
        return remote(
            plane_fin.at[z], plane_fin.at[slot], plane_fs.at[other], plane_fr.at[slot],
            at_plane(other),
        )

    for step in range(1, planes):
        plane_fin_copy(lax.rem(z + step, planes), z).start()

    def plane_copy(i, other, slot):
        kind = jnp.where(other > z, 0, 1)
        return remote(
            plane_sum.at[i, kind], from_planes.at[slot, i], plane_s.at[other * own + i],
            plane_r.at[slot * own + i], at_plane(other),
        )

    def sum_plane(i):
        head = me * own + i
        for step in range(1, chips):
            out_arrival(i, lax.rem(chip + step, chips)).wait_recv()
        kv = from_chips[0, i, 0].astype(F32)
        qd = from_chips[chips - 1, i, 1].astype(F32)
        for other in range(1, chips):
            kv = kv * jnp.exp(chip_fin[other, pl.ds(head, 1), :]) + from_chips[other, i, 0].astype(F32)
            back = chips - 1 - other
            qd = qd * jnp.exp(chip_fin[back, pl.ds(head, 1), :]) + from_chips[back, i, 1].astype(F32)
        plane_sum[i, 0] = kv.astype(BF16)
        plane_sum[i, 1] = qd.astype(BF16)
        for step in range(1, planes):
            plane_copy(i, lax.rem(z + step, planes), z).start()

    def back_copy(i, other):
        return remote(
            to_back.at[other, i], from_back.at[chip, i], back_s.at[other * own + i],
            back_r.at[chip * own + i], at_chip(other),
        )

    def back_arrival(i, other):
        return remote(
            to_back.at[other, i], from_back.at[other, i], back_s.at[other * own + i],
            back_r.at[other * own + i], at_chip(other),
        )

    def carry(i):
        head = me * own + i
        for step in range(1, planes):
            other = lax.rem(z + step, planes)
            plane_copy(i, other, other).wait_recv()
        kv = jnp.zeros((SIZE, SIZE), F32)
        qd = jnp.zeros((SIZE, SIZE), F32)
        for other in range(planes):
            factor = jnp.exp(plane_fin[other, pl.ds(head, 1), :])
            kv = jnp.where(other < z, kv * factor + from_planes[other, i].astype(F32), kv)
            back = planes - 1 - other
            factor = jnp.exp(plane_fin[back, pl.ds(head, 1), :])
            qd = jnp.where(back > z, qd * factor + from_planes[back, i].astype(F32), qd)
        for other in range(chips):
            to_back[other, i, 0] = kv.astype(BF16)
            back = chips - 1 - other
            to_back[back, i, 1] = qd.astype(BF16)
            if other < chips - 1:
                factor = jnp.exp(chip_fin[other, pl.ds(head, 1), :])
                kv = kv * factor + from_chips[other, i, 0].astype(F32)
                factor = jnp.exp(chip_fin[back, pl.ds(head, 1), :])
                qd = qd * factor + from_chips[back, i, 1].astype(F32)
        for step in range(1, chips):
            back_copy(i, lax.rem(chip + step, chips)).start()
        from_back[chip, i] = to_back[chip, i]

    def last_copy(i, other, side):
        head = (other * 2 + side) * own + i
        slot = other * own + i
        return remote(
            to_core.at[slot], states_ref.at[head], last_s.at[slot], last_r.at[slot], at_core()
        )

    def finish(i):
        @pl.loop(0, chips)
        def _(step):
            other = lax.rem(chip + step, chips)

            @pl.when(step > 0)
            def _():
                back_arrival(i, other).wait_recv()

            head = (other * 2 + core) * own + i
            slot = other * own + i
            mine = jnp.exp(own_fin[pl.ds(head, 1), :])
            theirs = jnp.exp(core_fin[pl.ds(head, 1), :])
            one = jnp.ones_like(mine)
            enter = from_back[other, i, 0].astype(F32)
            trail = from_back[other, i, 1].astype(F32)
            late = jnp.where(
                first_core, mine * enter + terms[head, 0],
                theirs * enter + from_core[slot, 0],
            )
            early = jnp.where(
                first_core, theirs * trail + from_core[slot, 1],
                mine * trail + terms[head, 1],
            )
            to_core[slot, 0] = jnp.where(first_core, late, enter).astype(BF16)
            to_core[slot, 1] = jnp.where(first_core, trail, early).astype(BF16)
            last_copy(i, other, core).start()
            states_ref[head, 0] = jnp.where(first_core, enter, late).astype(BF16)
            states_ref[head, 1] = jnp.where(first_core, early, trail).astype(BF16)

    events = []
    lead = min(2, own)
    for i in range(lead):
        events.append((sum_plane, i))
    for i in range(own):
        events.append((carry, i))
        if i + lead < own:
            events.append((sum_plane, i + lead))
    done = 0
    waited = False
    for at, (event, i) in enumerate(events):
        if event is carry and not waited:
            waited = True
            for step in range(1, planes):
                other = lax.rem(z + step, planes)
                plane_fin_copy(other, other).wait_recv()
        event(i)
        until = 8 * (at + 1) // len(events)
        for part in range(done, until):
            inside_chunk(part)
        done = until
    pl.loop(0, own)(finish)

    fin_copy.wait_send()
    for step in range(1, chips):
        chip_fin_copy(lax.rem(chip + step, chips), chip).wait_send()
    for step in range(1, planes):
        plane_fin_copy(lax.rem(z + step, planes), z).wait_send()

    @pl.loop(0, own)
    def _(i):
        @pl.loop(0, chips)
        def _(other):
            core_copy(i, other).wait_send()
            last_copy(i, other, core).wait_send()
            last_copy(i, other, 1 - core).wait_recv()

        @pl.loop(1, chips)
        def _(step):
            other = lax.rem(chip + step, chips)
            out_copy(i, other).wait_send()
            back_copy(i, other).wait_send()

        @pl.loop(1, planes)
        def _(step):
            plane_copy(i, lax.rem(z + step, planes), z).wait_send()


def carried_states(planes, devices, arrays):
    decay = arrays[-1]
    arrays = [pltpu.with_memory_space_constraint(item, pltpu.HBM) for item in arrays[:-1]] + [decay]
    heads = decay.shape[1]
    chips, own = devices // 2, heads // devices
    square = (SIZE, SIZE)
    dma = pltpu.SemaphoreType.DMA
    slots = chips * own
    return pl.pallas_call(
        functools.partial(states_kernel, planes, devices),
        out_shape=[jax.ShapeDtypeStruct((heads, 2) + square, BF16)]
        + [jax.ShapeDtypeStruct(arrays[0].shape, BF16)] * 4
        + [
            jax.ShapeDtypeStruct((heads,) + square, F32),
            jax.ShapeDtypeStruct((4, heads) + square, F32),
        ],
        in_specs=[pl.BlockSpec(memory_space=pltpu.HBM)] * 4
        + [pl.BlockSpec(memory_space=pltpu.VMEM)],
        out_specs=[pl.BlockSpec(memory_space=pltpu.VMEM)] * 7,
        scratch_shapes=[
            pltpu.VMEM((heads, SIZE), F32),
            pltpu.VMEM((heads, 2) + square, F32),
            pltpu.VMEM((slots, 2) + square, F32),
            pltpu.VMEM((chips, own, 2) + square, BF16),
            pltpu.VMEM((chips, own, 2) + square, BF16),
            pltpu.VMEM((own, 2) + square, BF16),
            pltpu.VMEM((planes, own) + square, BF16),
            pltpu.VMEM((chips, own, 2) + square, BF16),
            pltpu.VMEM((chips, own, 2) + square, BF16),
            pltpu.VMEM((slots, 2) + square, BF16),
            pltpu.VMEM((heads, SIZE), F32),
            pltpu.VMEM((heads, SIZE), F32),
            pltpu.VMEM((chips, heads, SIZE), F32),
            pltpu.VMEM((planes, heads, SIZE), F32),
            dma((4, devices, 2)), dma, dma, dma((chips,)), dma((chips,)), dma((planes,)), dma((planes,)),
            dma((slots,)), dma((slots,)), dma((slots,)), dma((slots,)),
            dma((planes * own,)), dma((planes * own,)),
            dma((slots,)), dma((slots,)), dma((slots,)), dma((slots,)),
        ],
        compiler_params=pltpu.CompilerParams(
            collective_id=0, has_side_effects=True, vmem_limit_bytes=20 * 2**20
        ),
    )(*arrays)


def block_kernel(
    group, states_ref, q_ref, k_ref, v_ref, g_ref, cumuls, local, o_ref, dq_ref, dk_ref, dv_ref
):
    for i in range(group):
        head = pl.program_id(0) * group + i
        columns = slice(i * SIZE, (i + 1) * SIZE)
        taken = pl.ds(pl.multiple_of(head * SIZE, SIZE), SIZE)
        query, key, value, grad = (ref[:, taken] for ref in (q_ref, k_ref, v_ref, g_ref))
        enter, trail = states_ref[head, 0], states_ref[head, 1]
        cumul = cumuls[head]
        forward = jnp.exp(cumul)
        backward = jnp.exp(cumul[-1:, :] - cumul)
        o_ref[:, columns] = (
            local[0, head] + forward * jnp.dot(query, enter, preferred_element_type=F32)
        ).astype(BF16)
        dq_ref[:, columns] = (local[1, head] + forward * over_columns(grad, enter)).astype(BF16)
        dk_ref[:, columns] = (local[2, head] + backward * over_columns(value, trail)).astype(BF16)
        dv_ref[:, columns] = (
            local[3, head] + backward * jnp.dot(key, trail, preferred_element_type=F32)
        ).astype(BF16)


def block_results(held):
    rows, features = held[1].shape
    group = 8
    return pl.pallas_call(
        functools.partial(block_kernel, group),
        grid=(features // (group * SIZE),),
        out_shape=[jax.ShapeDtypeStruct((rows, features), BF16)] * 4,
        in_specs=[pl.BlockSpec(memory_space=pltpu.VMEM)] * 7,
        out_specs=[pl.BlockSpec((rows, group * SIZE), lambda i: (0, i))] * 4,
        compiler_params=pltpu.CompilerParams(vmem_limit_bytes=8 * 2**20),
    )(*held)


def solution(mesh):
    planes, devices = mesh.shape["chain"], mesh.shape["inner"]

    def shards(*arrays):
        return tuple(block_results(carried_states(planes, devices, arrays)))

    spec = P(("chain", "inner"), None)
    return jax.shard_map(
        shards, mesh=mesh, in_specs=(spec,) * 5, out_specs=(spec,) * 4, check_vma=False
    )
```

profile of v0, /device:TPU:0, one launch (start us, length us, event | category | flops | bytes accessed | tf_op | source)
XLA Modules:
  0.0 41.8 jit_solution(3085019303697599624)
XLA Ops:
  0.6 0.8 %copy.9.decay_ref = bf16[128,32]{1,0:T(8,128)(2,1)S(1)} copy(bf16[128,32]{0,1:T(8,128)(2,1)} %param.9) | data formatting | bytes 16384 | tf_op args[4]
  1.4 36.6 %shard_map.84 = (bf16[32,2,128,128]{3,2,1,0:T(8,128)(2,1)S(1)}, bf16[128,4096]{1,0:T(8,128)(2,1)S(1)}, bf16[128,4096]{1,0:T(8,128)(2,1)S(1)}, bf16[128,4096]{1,0...) custom-call(bf16[128,4096]{1,0:T(8,128)(2,1)} %q_any.1, ...), custom_call_target="tpu_custom_call" | custom-call | tf_op jit(solution)/shard_map/pallas_call | solution.py:424
  38.0 3.8 %shard_map.85 = (bf16[128,4096]{1,0:T(8,128)(2,1)}, bf16[128,4096]{1,0:T(8,128)(2,1)}, bf16[128,4096]{1,0:T(8,128)(2,1)}, bf16[128,4096]{1,0:T(8,128)(2,1)}) custom-call(bf16[32,2,128,128]{3,2,1,0:T(8,128)(2,1)S(1)} %get-tuple-element.11.states_ref, bf16[128,4096]{1,0:T(8,128)(2,1)S(1)} %get-tuple-element.12.q_ref, ...), custom_call_target="tpu_custom_call" | custom-call | tf_op jit(solution)/shard_map/pallas_call | solution.py:486
where the time goes:
time: 42 us; the launch traced here: 41.8 us
  Pallas kernels  40.3 us (96%)
  local copies, waits for them, and re-layouts  0.81 us (2%)
  between operations  0.64 us (2%)
    pallas_call x1, Pallas kernels, carried_states(): pl.pallas_call(functools.partial(states_kernel, planes, devices), out_sha...  36.6 us
    pallas_call x1, Pallas kernels, block_results(): pl.pallas_call(functools.partial(block_kernel, group), grid=(features //...  3.76 us

commit v1 on v0

v1 whole, which is shorter than its diff:
```python
import functools

import jax
import jax.numpy as jnp
from jax import lax
from jax.experimental import pallas as pl
from jax.experimental.pallas import tpu as pltpu
from jax.sharding import PartitionSpec as P

SIZE = 128
F32 = jnp.float32
BF16 = jnp.bfloat16
MESH = pl.DeviceIdType.MESH


def lower_triangle(rows):
    row = lax.broadcasted_iota(jnp.int32, (rows, rows), 0)
    column = lax.broadcasted_iota(jnp.int32, (rows, rows), 1)
    return row >= column


def over_rows(left, right):
    return lax.dot_general(left, right, (((0,), (0,)), ((), ())), preferred_element_type=F32)


def over_columns(left, right):
    return lax.dot_general(left, right, (((1,), (1,)), ((), ())), preferred_element_type=F32)


def dot(left, right):
    return jnp.dot(left, right, preferred_element_type=F32)


def plan(rounds, parts):
    ready = []
    for i in range(rounds):
        ready.append((11.0 + 1.4 * i, 0.15, "sum", i))
        ready.append((16.2 + 1.4 * i, 0.35, "carry", i))
        ready.append((21.7 + 1.4 * i, 0.3, "pass", i))
        ready.append((22.9 + 1.4 * i, 0.7, "final", i))
    ready.append((9.6, 0.1, "planes", 0))
    ready.sort()
    order, now, part = [], 9.2, 0
    while ready:
        if ready[0][0] > now + 0.1 and part < parts:
            order.append(("inside", part))
            now += 8.6 / parts
            part += 1
            continue
        at, length, step, i = ready.pop(0)
        if step == "final":
            while part < min(parts, -(-parts * (i + 1) // rounds)):
                order.append(("inside", part))
                now += 8.6 / parts
                part += 1
        order.append((step, i))
        now = max(now, at) + length
    return order


def main_kernel(
    planes, devices, q_any, k_any, v_any, g_any, d_any,
    o_ref, dq_ref, dk_ref, dv_ref,
    q_ref, k_ref, v_ref, g_ref, d_ref, decay_rows, forward_rows, backward_rows,
    forward, backward, local, terms, from_core,
    to_chips, from_chips, plane_sum, from_planes, to_back, raw, states,
    own_fin, core_fin, chip_fin, plane_fin,
    load_s, decay_s, fin_s, fin_r, chip_fs, chip_fr, plane_fs, plane_fr,
    core_s, core_r, out_s, out_r, plane_s, plane_r, back_s, back_r, last_s, last_r,
):
    heads, rows = d_any.shape
    chips = devices // 2
    own = heads // chips
    z = lax.axis_index("chain")
    me = lax.axis_index("inner")
    chip, core = me // 2, lax.rem(me, 2)
    kind = 1 - core
    ahead = core == 1

    def place(j):
        return jnp.where(ahead, j, chips - 1 - j)

    def level(j):
        return jnp.where(ahead, j, planes - 1 - j)

    depth = level(z)

    def at_core():
        return (z, chip * 2 + 1 - core)

    def at_chip(other):
        return (z, other * 2 + core)

    def at_plane(other):
        return (other, me)

    def remote(src, dst, send, recv, to):
        return pltpu.make_async_remote_copy(
            src_ref=src, dst_ref=dst, send_sem=send, recv_sem=recv, device_id=to, device_id_type=MESH
        )

    def columns(head):
        return pl.ds(pl.multiple_of(head * SIZE, SIZE), SIZE)

    def loads(i):
        taken = pl.ds(pl.multiple_of(i * (chips * SIZE), SIZE), chips * SIZE)
        pairs = ((k_any, k_ref), (v_any, v_ref), (q_any, q_ref), (g_any, g_ref))
        return [
            pltpu.make_async_copy(src.at[:, taken], dst.at[:, taken], load_s.at[j, i])
            for j, (src, dst) in enumerate(pairs)
        ]

    decay_load = pltpu.make_async_copy(d_any, d_ref, decay_s)
    decay_load.start()

    @pl.loop(0, own)
    def _(i):
        for copy in loads(i):
            copy.start()

    barrier = pltpu.get_barrier_semaphore()
    for step in range(1, planes):
        pl.semaphore_signal(
            barrier, inc=1, device_id=at_plane(lax.rem(z + step, planes)), device_id_type=MESH
        )
    for step in range(1, chips):
        pl.semaphore_signal(
            barrier, inc=1, device_id=at_chip(lax.rem(chip + step, chips)), device_id_type=MESH
        )
    pl.semaphore_signal(barrier, inc=1, device_id=at_core(), device_id_type=MESH)

    lower = lower_triangle(rows)
    row = lax.broadcasted_iota(jnp.int32, (rows, rows), 0)
    column = lax.broadcasted_iota(jnp.int32, (rows, rows), 1)
    upto = (row <= column).astype(F32).astype(BF16)
    after = (row > column).astype(F32).astype(BF16)
    ones = jnp.ones((rows, SIZE), BF16)

    decay_load.wait()
    decay = d_ref[...]
    decay_rows[...] = decay.astype(F32)
    fin = dot(decay, ones)
    cumul = dot(decay, upto)
    own_fin[...] = fin
    forward_rows[...] = jnp.exp(cumul)
    backward_rows[...] = jnp.exp(fin - cumul)

    def make_terms(head):
        taken = columns(head)
        keys = k_ref[:, taken].T.astype(F32) * backward_rows[pl.ds(head, 1), :]
        terms[0, head] = dot(keys.astype(BF16), v_ref[:, taken])
        queries = q_ref[:, taken].T.astype(F32) * forward_rows[pl.ds(head, 1), :]
        terms[1, head] = dot(queries.astype(BF16), g_ref[:, taken])

    @pl.loop(0, own)
    def _(i):
        for copy in loads(i):
            copy.wait()
        for o in range(chips):
            make_terms(i * chips + o)

    def inside(head):
        taken = columns(head)
        query, key, value, grad = (ref[:, taken] for ref in (q_ref, k_ref, v_ref, g_ref))
        picked = jnp.where(lower, decay_rows[pl.ds(head, 1), :], 0.0).astype(BF16)
        spans = dot(picked, jnp.concatenate([after, ones], axis=1))
        weights = jnp.where(lower, jnp.exp(spans[:, :rows]), 0.0)
        sums = spans[:, rows:]
        forward[head] = jnp.exp(sums)
        backward[head] = jnp.exp(own_fin[pl.ds(head, 1), :] - sums)
        probs = (over_columns(query, key) * weights).astype(BF16)
        grows = (over_columns(grad, value) * weights).astype(BF16)
        local[0, head] = dot(probs, value)
        local[1, head] = dot(grows, key)
        local[2, head] = over_rows(grows, query)
        local[3, head] = over_rows(probs, grad)

    pl.semaphore_wait(barrier, chips + planes - 1)

    fin_copy = remote(own_fin, core_fin, fin_s, fin_r, at_core())
    fin_copy.start()

    def core_copy(head):
        return remote(
            terms.at[core, head], from_core.at[head], core_s.at[head], core_r.at[head], at_core()
        )

    @pl.loop(0, heads)
    def _(head):
        core_copy(head).start()

    fin_copy.wait_recv()
    chip_fin[chip] = own_fin[...] + core_fin[...]

    def chip_fin_copy(other, slot):
        return remote(
            chip_fin.at[chip], chip_fin.at[slot], chip_fs.at[other], chip_fr.at[slot], at_chip(other)
        )

    def out_copy(i, other):
        to, slot = i * chips + other, i * chips + chip
        return remote(
            to_chips.at[to], from_chips.at[slot], out_s.at[to], out_r.at[slot], at_chip(other)
        )

    def out_arrival(i, other):
        to = i * chips + other
        return remote(
            to_chips.at[to], from_chips.at[to], out_s.at[to], out_r.at[to], at_chip(other)
        )

    def combine(i):
        for step in range(chips):
            other = lax.rem(chip + 1 + step, chips)
            head = i * chips + other
            core_copy(head).wait_recv()
            factor = jnp.exp(own_fin[pl.ds(head, 1), :])
            total = (terms[kind, head] + factor * from_core[head]).astype(BF16)
            if step < chips - 1:
                to_chips[head] = total
            else:
                from_chips[head] = total
            if step > 0:
                out_copy(i, lax.rem(chip + step, chips)).start()

    combine(0)
    for step in range(1, chips):
        chip_fin_copy(lax.rem(chip + step, chips), chip).start()
    pl.loop(1, own)(combine)

    def plane_fin_copy(other, slot):
        return remote(
            plane_fin.at[z], plane_fin.at[slot], plane_fs.at[other], plane_fr.at[slot],
            at_plane(other),
        )

    def planes_step(_):
        for step in range(1, chips):
            other = lax.rem(chip + step, chips)
            chip_fin_copy(other, other).wait_recv()
        total = chip_fin[0]
        for other in range(1, chips):
            total = total + chip_fin[other]
        plane_fin[z] = total
        for step in range(1, planes):
            plane_fin_copy(lax.rem(z + step, planes), z).start()

    def plane_copy(i, other, slot):
        return remote(
            plane_sum.at[i], from_planes.at[slot, i], plane_s.at[other * own + i],
            plane_r.at[slot * own + i], at_plane(other),
        )

    def factor_of(fins, at, head):
        return jnp.exp(fins[at, pl.ds(head, 1), :])

    def sum_step(i):
        head = i * chips + chip
        for step in range(1, chips):
            out_arrival(i, lax.rem(chip + step, chips)).wait_recv()

        @pl.when(depth < planes - 1)
        def _():
            total = from_chips[i * chips + place(0)].astype(F32)
            for j in range(1, chips):
                at = place(j)
                total = total * factor_of(chip_fin, at, head) + from_chips[i * chips + at].astype(F32)
            plane_sum[i] = total.astype(BF16)

            @pl.loop(0, planes - 1 - depth)
            def _(j):
                plane_copy(i, level(planes - 1 - j), z).start()

    def back_copy(i, other):
        to, slot = i * chips + other, i * chips + chip
        return remote(
            to_back.at[to], raw.at[slot], back_s.at[to], back_r.at[slot], at_chip(other)
        )

    def back_arrival(i, other):
        to = i * chips + other
        return remote(to_back.at[to], raw.at[to], back_s.at[to], back_r.at[to], at_chip(other))

    def carry_step(i):
        head = i * chips + chip
        if i == 0:
            for step in range(1, planes):
                other = lax.rem(z + step, planes)
                plane_fin_copy(other, other).wait_recv()

        def add_plane(j, state):
            at = level(j)
            plane_copy(i, at, at).wait_recv()
            return state * factor_of(plane_fin, at, head) + from_planes[at, i].astype(F32)

        state = lax.fori_loop(0, depth, add_plane, jnp.zeros((SIZE, SIZE), F32))
        for j in range(chips):
            at = place(j)
            to_back[i * chips + at] = state.astype(BF16)
            if j < chips - 1:
                state = state * factor_of(chip_fin, at, head) + from_chips[i * chips + at].astype(F32)
        for step in range(1, chips):
            back_copy(i, lax.rem(chip + step, chips)).start()
        raw[head] = to_back[head]

    def last_copy(head):
        return remote(
            raw.at[head], states.at[kind, head], last_s.at[head], last_r.at[head], at_core()
        )

    def last_arrival(head):
        return remote(
            raw.at[head], states.at[core, head], last_s.at[head], last_r.at[head], at_core()
        )

    def pass_step(i):
        last_copy(i * chips + chip).start()
        for step in range(1, chips):
            other = lax.rem(chip + step, chips)
            back_arrival(i, other).wait_recv()
            last_copy(i * chips + other).start()
        for o in range(chips):
            head = i * chips + o
            factor = jnp.exp(core_fin[pl.ds(head, 1), :])
            states[kind, head] = (factor * raw[head].astype(F32) + from_core[head]).astype(BF16)

    def final_step(i):
        for o in range(chips):
            last_arrival(i * chips + o).wait_recv()
        for o in range(chips):
            head = i * chips + o
            taken = columns(head)
            query, key, value, grad = (ref[:, taken] for ref in (q_ref, k_ref, v_ref, g_ref))
            enter, trail = states[0, head], states[1, head]
            front, behind = forward[head], backward[head]
            o_ref[:, taken] = (local[0, head] + front * dot(query, enter)).astype(BF16)
            dq_ref[:, taken] = (local[1, head] + front * over_columns(grad, enter)).astype(BF16)
            dk_ref[:, taken] = (local[2, head] + behind * over_columns(value, trail)).astype(BF16)
            dv_ref[:, taken] = (local[3, head] + behind * dot(key, trail)).astype(BF16)

    parts = heads // 2

    def inside_step(part):
        for j in range(2):
            inside(part * 2 + j)

    steps = {
        "planes": planes_step, "sum": sum_step, "carry": carry_step, "pass": pass_step,
        "final": final_step, "inside": inside_step,
    }
    for step, i in plan(own, parts):
        steps[step](i)

    fin_copy.wait_send()
    for step in range(1, chips):
        chip_fin_copy(lax.rem(chip + step, chips), chip).wait_send()
    for step in range(1, planes):
        plane_fin_copy(lax.rem(z + step, planes), z).wait_send()

    @pl.loop(0, heads)
    def _(head):
        core_copy(head).wait_send()
        last_copy(head).wait_send()

    @pl.loop(0, own)
    def _(i):
        for step in range(1, chips):
            other = lax.rem(chip + step, chips)
            out_copy(i, other).wait_send()
            back_copy(i, other).wait_send()

        @pl.loop(0, planes - 1 - depth)
        def _(j):
            plane_copy(i, level(planes - 1 - j), z).wait_send()


def computed(planes, devices, arrays):
    decay = pltpu.with_memory_space_constraint(arrays[-1].T, pltpu.HBM)
    arrays = [pltpu.with_memory_space_constraint(item, pltpu.HBM) for item in arrays[:-1]] + [decay]
    heads, rows = decay.shape
    chips = devices // 2
    own = heads // chips
    square = (SIZE, SIZE)
    wide = arrays[0].shape
    dma = pltpu.SemaphoreType.DMA
    return pl.pallas_call(
        functools.partial(main_kernel, planes, devices),
        out_shape=[jax.ShapeDtypeStruct(wide, BF16)] * 4,
        in_specs=[pl.BlockSpec(memory_space=pltpu.HBM)] * 5,
        out_specs=[pl.BlockSpec(memory_space=pltpu.VMEM)] * 4,
        scratch_shapes=[pltpu.VMEM(wide, BF16)] * 4
        + [
            pltpu.VMEM((heads, rows), BF16),
            pltpu.VMEM((heads, rows), F32),
            pltpu.VMEM((heads, rows), F32),
            pltpu.VMEM((heads, rows), F32),
            pltpu.VMEM((heads, rows, SIZE), F32),
            pltpu.VMEM((heads, rows, SIZE), F32),
            pltpu.VMEM((4, heads) + square, F32),
            pltpu.VMEM((2, heads) + square, F32),
            pltpu.VMEM((heads,) + square, F32),
            pltpu.VMEM((heads,) + square, BF16),
            pltpu.VMEM((heads,) + square, BF16),
            pltpu.VMEM((own,) + square, BF16),
            pltpu.VMEM((planes, own) + square, BF16),
            pltpu.VMEM((heads,) + square, BF16),
            pltpu.VMEM((heads,) + square, BF16),
            pltpu.VMEM((2, heads) + square, BF16),
            pltpu.VMEM((heads, SIZE), F32),
            pltpu.VMEM((heads, SIZE), F32),
            pltpu.VMEM((chips, heads, SIZE), F32),
            pltpu.VMEM((planes, heads, SIZE), F32),
            dma((4, own)), dma, dma, dma, dma((chips,)), dma((chips,)), dma((planes,)), dma((planes,)),
            dma((heads,)), dma((heads,)), dma((heads,)), dma((heads,)),
            dma((planes * own,)), dma((planes * own,)),
            dma((heads,)), dma((heads,)), dma((heads,)), dma((heads,)),
        ],
        compiler_params=pltpu.CompilerParams(
            collective_id=0, has_side_effects=True, vmem_limit_bytes=48 * 2**20
        ),
    )(*arrays)


def store_kernel(o_ref, dq_ref, dk_ref, dv_ref, o_out, dq_out, dk_out, dv_out, store_s):
    pairs = ((o_ref, o_out), (dq_ref, dq_out), (dk_ref, dk_out), (dv_ref, dv_out))
    copies = [pltpu.make_async_copy(src, dst, store_s.at[j]) for j, (src, dst) in enumerate(pairs)]
    for copy in copies:
        copy.start()
    for copy in copies:
        copy.wait()


def stored(results):
    return pl.pallas_call(
        store_kernel,
        out_shape=[jax.ShapeDtypeStruct(item.shape, BF16) for item in results],
        in_specs=[pl.BlockSpec(memory_space=pltpu.VMEM)] * 4,
        out_specs=[pl.BlockSpec(memory_space=pltpu.HBM)] * 4,
        scratch_shapes=[pltpu.SemaphoreType.DMA((4,))],
        compiler_params=pltpu.CompilerParams(vmem_limit_bytes=2 * 2**20),
    )(*results)


def solution(mesh):
    planes, devices = mesh.shape["chain"], mesh.shape["inner"]

    def shards(*arrays):
        return tuple(stored(computed(planes, devices, arrays)))

    spec = P(("chain", "inner"), None)
    return jax.shard_map(
        shards, mesh=mesh, in_specs=(spec,) * 5, out_specs=(spec,) * 4, check_vma=False
    )
```

time: 42 us -> 42 us (level)
  local copies, waits for them, and re-layouts: 0.81 us -> 0 us
  Pallas kernels: 40.3 us -> 41.1 us
    unnamed x1 -> x0, local copies, waits for them, and re-layouts: 0.81 us -> none
    pallas_call x2, Pallas kernels: 40.3 us -> 41.1 us  [the longest x1 39.1 us: computed(): pl.pallas_call(functools.partial(main_kernel, planes, devices), out_shape...]
where the time goes in v1:
time: 42 us; the launch traced here: 41.7 us
  Pallas kernels  41.1 us (98%)
  between operations  0.64 us (2%)
    pallas_call x1, Pallas kernels, computed(): pl.pallas_call(functools.partial(main_kernel, planes, devices), out_shape...  39.1 us
    pallas_call x1, Pallas kernels, stored(): pl.pallas_call(store_kernel, out_shape=[jax.ShapeDtypeStruct(item.shape,...  2.04 us

profile of v1, /device:TPU:0, one launch (start us, length us, event | category | flops | bytes accessed | tf_op | source)
XLA Modules:
  0.0 41.7 jit_solution(11991471987369864800)
XLA Ops:
  0.6 39.1 %shard_map.84 = (bf16[128,4096]{1,0:T(8,128)(2,1)S(1)}, bf16[128,4096]{1,0:T(8,128)(2,1)S(1)}, bf16[128,4096]{1,0:T(8,128)(2,1)S(1)}, bf16[128,4096]{1,0:T(8,128)(2,1)S(1)}) custom-call(bf16[128,4096]{1,0:T(8,128)(2,1)} %q_any.1, bf16[128,4096]{1,0:T(8,128)(2,1)} %k_any.1, bf16[128,4096]{1,0:T(8,128)(2,1)} %v_any.1, bf16[128,4096]{1,0:T(8,128)(2,1)} %g_any.1, ...), custom_call_target="tpu_custom_call" | custom-call | tf_op jit(solution)/shard_map/pallas_call | solution.py:386
  39.7 2.0 %shard_map.85 = (bf16[128,4096]{1,0:T(8,128)(2,1)}, bf16[128,4096]{1,0:T(8,128)(2,1)}, bf16[128,4096]{1,0:T(8,128)(2,1)}, bf16[128,4096]{1,0:T(8,128)(2,1)}) custom-call(bf16[128,4096]{1,0:T(8,128)(2,1)S(1)} %get-tuple-element.8.o_ref, bf16[128,4096]{1,0:T(8,128)(2,1)S(1)} %get-tuple-element.9.dq_ref, bf16[128,4096]{1,0:T(8,128)(2,1)S(1)} %get-tuple-element.10.dk_ref, ...), custom_call_target="tpu_custom_call" | custom-call | tf_op jit(solution)/shard_map/pallas_call | solution.py:434

commit v2 on v1

--- a/solution.py
+++ b/solution.py
@@ -61,12 +61,12 @@
 def main_kernel(
     planes, devices, q_any, k_any, v_any, g_any, d_any,
     o_ref, dq_ref, dk_ref, dv_ref,
-    q_ref, k_ref, v_ref, g_ref, d_ref, decay_rows, forward_rows, backward_rows,
+    held, d_ref, decay_rows, forward_rows, backward_rows,
     forward, backward, local, terms, from_core,
     to_chips, from_chips, plane_sum, from_planes, to_back, raw, states,
     own_fin, core_fin, chip_fin, plane_fin,
     load_s, decay_s, fin_s, fin_r, chip_fs, chip_fr, plane_fs, plane_fr,
-    core_s, core_r, out_s, out_r, plane_s, plane_r, back_s, back_r, last_s, last_r,
+    core_s, first_r, core_r, out_s, out_r, plane_s, plane_r, back_s, back_r, last_s, last_r,
 ):
     heads, rows = d_any.shape
     chips = devices // 2
@@ -104,11 +104,17 @@
 
     def loads(i):
         taken = pl.ds(pl.multiple_of(i * (chips * SIZE), SIZE), chips * SIZE)
-        pairs = ((k_any, k_ref), (v_any, v_ref), (q_any, q_ref), (g_any, g_ref))
         return [
-            pltpu.make_async_copy(src.at[:, taken], dst.at[:, taken], load_s.at[j, i])
-            for j, (src, dst) in enumerate(pairs)
+            pltpu.make_async_copy(src.at[:, taken], held.at[j, :, taken], load_s.at[i])
+            for j, src in enumerate((q_any, k_any, v_any, g_any))
         ]
+
+    def wait_loads(i):
+        taken = pl.ds(pl.multiple_of(i * (chips * SIZE), SIZE), chips * SIZE)
+        part = held.at[:, :, taken]
+        pltpu.make_async_copy(part, part, load_s.at[i]).wait()
+
+    q_ref, k_ref, v_ref, g_ref = (held.at[j] for j in range(4))
 
     decay_load = pltpu.make_async_copy(d_any, d_ref, decay_s)
     decay_load.start()
@@ -154,8 +160,7 @@
 
     @pl.loop(0, own)
     def _(i):
-        for copy in loads(i):
-            copy.wait()
+        wait_loads(i)
         for o in range(chips):
             make_terms(i * chips + o)
 
@@ -180,40 +185,45 @@
     fin_copy = remote(own_fin, core_fin, fin_s, fin_r, at_core())
     fin_copy.start()
 
-    def core_copy(head):
-        return remote(
-            terms.at[core, head], from_core.at[head], core_s.at[head], core_r.at[head], at_core()
-        )
-
-    @pl.loop(0, heads)
-    def _(head):
-        core_copy(head).start()
+    def core_copy(begin, count, recv):
+        taken = pl.ds(begin, count)
+        return remote(terms.at[core, taken], from_core.at[taken], core_s, recv, at_core())
+
+    def first_copy(o):
+        return core_copy(o, 1, first_r.at[o])
+
+    def round_copy(i):
+        return core_copy(i * chips, chips, core_r.at[i - 1])
+
+    for step in range(chips):
+        first_copy(lax.rem(chip + 1 + step, chips)).start()
+    for i in range(1, own):
+        round_copy(i).start()
 
     fin_copy.wait_recv()
     chip_fin[chip] = own_fin[...] + core_fin[...]
 
     def chip_fin_copy(other, slot):
         return remote(
-            chip_fin.at[chip], chip_fin.at[slot], chip_fs.at[other], chip_fr.at[slot], at_chip(other)
+            chip_fin.at[chip], chip_fin.at[slot], chip_fs, chip_fr, at_chip(other)
         )
 
     def out_copy(i, other):
         to, slot = i * chips + other, i * chips + chip
-        return remote(
-            to_chips.at[to], from_chips.at[slot], out_s.at[to], out_r.at[slot], at_chip(other)
-        )
-
-    def out_arrival(i, other):
-        to = i * chips + other
-        return remote(
-            to_chips.at[to], from_chips.at[to], out_s.at[to], out_r.at[to], at_chip(other)
-        )
+        return remote(to_chips.at[to], from_chips.at[slot], out_s, out_r.at[i], at_chip(other))
+
+    def out_copies(count, recv):
+        taken = pl.ds(0, count)
+        return remote(to_chips.at[taken], from_chips.at[taken], out_s, recv, at_core())
 
     def combine(i):
+        if i > 0:
+            round_copy(i).wait_recv()
         for step in range(chips):
             other = lax.rem(chip + 1 + step, chips)
             head = i * chips + other
-            core_copy(head).wait_recv()
+            if i == 0:
+                first_copy(other).wait_recv()
             factor = jnp.exp(own_fin[pl.ds(head, 1), :])
             total = (terms[kind, head] + factor * from_core[head]).astype(BF16)
             if step < chips - 1:
@@ -226,18 +236,17 @@
     combine(0)
     for step in range(1, chips):
         chip_fin_copy(lax.rem(chip + step, chips), chip).start()
-    pl.loop(1, own)(combine)
+    for i in range(1, own):
+        combine(i)
 
     def plane_fin_copy(other, slot):
         return remote(
-            plane_fin.at[z], plane_fin.at[slot], plane_fs.at[other], plane_fr.at[slot],
-            at_plane(other),
+            plane_fin.at[z], plane_fin.at[slot], plane_fs, plane_fr, at_plane(other),
         )
 
     def planes_step(_):
-        for step in range(1, chips):
-            other = lax.rem(chip + step, chips)
-            chip_fin_copy(other, other).wait_recv()
+        taken = chip_fin.at[pl.ds(0, chips - 1)]
+        remote(taken, taken, chip_fs, chip_fr, at_core()).wait_recv()
         total = chip_fin[0]
         for other in range(1, chips):
             total = total + chip_fin[other]
@@ -247,8 +256,7 @@
 
     def plane_copy(i, other, slot):
         return remote(
-            plane_sum.at[i], from_planes.at[slot, i], plane_s.at[other * own + i],
-            plane_r.at[slot * own + i], at_plane(other),
+            plane_sum.at[i], from_planes.at[slot, i], plane_s, plane_r.at[i], at_plane(other)
         )
 
     def factor_of(fins, at, head):
@@ -256,8 +264,7 @@
 
     def sum_step(i):
         head = i * chips + chip
-        for step in range(1, chips):
-            out_arrival(i, lax.rem(chip + step, chips)).wait_recv()
+        out_copies(chips - 1, out_r.at[i]).wait_recv()
 
         @pl.when(depth < planes - 1)
         def _():
@@ -273,24 +280,25 @@
 
     def back_copy(i, other):
         to, slot = i * chips + other, i * chips + chip
-        return remote(
-            to_back.at[to], raw.at[slot], back_s.at[to], back_r.at[slot], at_chip(other)
-        )
-
-    def back_arrival(i, other):
-        to = i * chips + other
-        return remote(to_back.at[to], raw.at[to], back_s.at[to], back_r.at[to], at_chip(other))
+        return remote(to_back.at[to], raw.at[slot], back_s, back_r.at[i], at_chip(other))
+
+    def back_copies(count, recv):
+        taken = pl.ds(0, count)
+        return remote(to_back.at[taken], raw.at[taken], back_s, recv, at_core())
 
     def carry_step(i):
         head = i * chips + chip
         if i == 0:
-            for step in range(1, planes):
-                other = lax.rem(z + step, planes)
-                plane_fin_copy(other, other).wait_recv()
+            taken = plane_fin.at[pl.ds(0, planes - 1)]
+            remote(taken, taken, plane_fs, plane_fr, at_core()).wait_recv()
+        for count in range(1, planes):
+            @pl.when(depth == count)
+            def _():
+                taken = from_planes.at[pl.ds(0, count), i]
+                remote(taken, taken, plane_s, plane_r.at[i], at_core()).wait_recv()
 
         def add_plane(j, state):
             at = level(j)
-            plane_copy(i, at, at).wait_recv()
             return state * factor_of(plane_fin, at, head) + from_planes[at, i].astype(F32)
 
         state = lax.fori_loop(0, depth, add_plane, jnp.zeros((SIZE, SIZE), F32))
@@ -303,30 +311,20 @@
             back_copy(i, lax.rem(chip + step, chips)).start()
         raw[head] = to_back[head]
 
-    def last_copy(head):
-        return remote(
-            raw.at[head], states.at[kind, head], last_s.at[head], last_r.at[head], at_core()
-        )
-
-    def last_arrival(head):
-        return remote(
-            raw.at[head], states.at[core, head], last_s.at[head], last_r.at[head], at_core()
-        )
+    def last_copy(i):
+        taken = pl.ds(i * chips, chips)
+        return remote(raw.at[taken], states.at[kind, taken], last_s, last_r.at[i], at_core())
 
     def pass_step(i):
-        last_copy(i * chips + chip).start()
-        for step in range(1, chips):
-            other = lax.rem(chip + step, chips)
-            back_arrival(i, other).wait_recv()
-            last_copy(i * chips + other).start()
+        back_copies(chips - 1, back_r.at[i]).wait_recv()
+        last_copy(i).start()
         for o in range(chips):
             head = i * chips + o
             factor = jnp.exp(core_fin[pl.ds(head, 1), :])
             states[kind, head] = (factor * raw[head].astype(F32) + from_core[head]).astype(BF16)
 
     def final_step(i):
-        for o in range(chips):
-            last_arrival(i * chips + o).wait_recv()
+        last_copy(i).wait_recv()
         for o in range(chips):
             head = i * chips + o
             taken = columns(head)
@@ -352,26 +350,19 @@
         steps[step](i)
 
     fin_copy.wait_send()
-    for step in range(1, chips):
-        chip_fin_copy(lax.rem(chip + step, chips), chip).wait_send()
-    for step in range(1, planes):
-        plane_fin_copy(lax.rem(z + step, planes), z).wait_send()
-
-    @pl.loop(0, heads)
-    def _(head):
-        core_copy(head).wait_send()
-        last_copy(head).wait_send()
-
-    @pl.loop(0, own)
-    def _(i):
-        for step in range(1, chips):
-            other = lax.rem(chip + step, chips)
-            out_copy(i, other).wait_send()
-            back_copy(i, other).wait_send()
-
-        @pl.loop(0, planes - 1 - depth)
-        def _(j):
-            plane_copy(i, level(planes - 1 - j), z).wait_send()
+    taken = chip_fin.at[pl.ds(0, chips - 1)]
+    remote(taken, taken, chip_fs, chip_fr, at_core()).wait_send()
+    taken = plane_fin.at[pl.ds(0, planes - 1)]
+    remote(taken, taken, plane_fs, plane_fr, at_core()).wait_send()
+    core_copy(0, heads, core_r.at[0]).wait_send()
+    out_copies(own * (chips - 1), out_r.at[0]).wait_send()
+    back_copies(own * (chips - 1), back_r.at[0]).wait_send()
+    remote(raw, states.at[kind], last_s, last_r.at[0], at_core()).wait_send()
+    for count in range(1, planes):
+        @pl.when(planes - 1 - depth == count)
+        def _():
+            taken = from_planes.at[pl.ds(0, count)]
+            remote(taken, taken, plane_s, plane_r.at[0], at_core()).wait_send()
 
 
 def computed(planes, devices, arrays):
@@ -388,8 +379,8 @@
         out_shape=[jax.ShapeDtypeStruct(wide, BF16)] * 4,
         in_specs=[pl.BlockSpec(memory_space=pltpu.HBM)] * 5,
         out_specs=[pl.BlockSpec(memory_space=pltpu.VMEM)] * 4,
-        scratch_shapes=[pltpu.VMEM(wide, BF16)] * 4
-        + [
+        scratch_shapes=[
+            pltpu.VMEM((4,) + wide, BF16),
             pltpu.VMEM((heads, rows), BF16),
             pltpu.VMEM((heads, rows), F32),
             pltpu.VMEM((heads, rows), F32),
@@ -410,10 +401,9 @@
             pltpu.VMEM((heads, SIZE), F32),
             pltpu.VMEM((chips, heads, SIZE), F32),
             pltpu.VMEM((planes, heads, SIZE), F32),
-            dma((4, own)), dma, dma, dma, dma((chips,)), dma((chips,)), dma((planes,)), dma((planes,)),
-            dma((heads,)), dma((heads,)), dma((heads,)), dma((heads,)),
-            dma((planes * own,)), dma((planes * own,)),
-            dma((heads,)), dma((heads,)), dma((heads,)), dma((heads,)),
+            dma((own,)), dma, dma, dma, dma, dma, dma, dma,
+            dma, dma((chips,)), dma((own,)), dma, dma((own,)), dma, dma((own,)),
+            dma, dma((own,)), dma, dma((own,)),
         ],
         compiler_params=pltpu.CompilerParams(
             collective_id=0, has_side_effects=True, vmem_limit_bytes=48 * 2**20

time: 42 us -> 38.7 us (0.921)
  Pallas kernels: 41.1 us -> 37.8 us
    pallas_call x1, Pallas kernels: 39.1 us -> 35.8 us  [computed(): pl.pallas_call(functools.partial(main_kernel, planes, devices), out_shape...]
where the time goes in v2:
time: 38.7 us; the launch traced here: 38.5 us
  Pallas kernels  37.8 us (98%)
  between operations  0.64 us (2%)
    pallas_call x1, Pallas kernels, computed(): pl.pallas_call(functools.partial(main_kernel, planes, devices), out_shape...  35.8 us
    pallas_call x1, Pallas kernels, stored(): pl.pallas_call(store_kernel, out_shape=[jax.ShapeDtypeStruct(item.shape,...  2.04 us

profile of v2, /device:TPU:0, one launch (start us, length us, event | category | flops | bytes accessed | tf_op | source)
XLA Modules:
  0.0 38.5 jit_solution(9608934431452156827)
XLA Ops:
  0.6 35.8 %shard_map.84 = (bf16[128,4096]{1,0:T(8,128)(2,1)S(1)}, bf16[128,4096]{1,0:T(8,128)(2,1)S(1)}, bf16[128,4096]{1,0:T(8,128)(2,1)S(1)}, bf16[128,4096]{1,0:T(8,128)(2,1)S(1)}) custom-call(bf16[128,4096]{1,0:T(8,128)(2,1)} %q_any.1, bf16[128,4096]{1,0:T(8,128)(2,1)} %k_any.1, bf16[128,4096]{1,0:T(8,128)(2,1)} %v_any.1, bf16[128,4096]{1,0:T(8,128)(2,1)} %g_any.1, ...), custom_call_target="tpu_custom_call" | custom-call | tf_op jit(solution)/shard_map/pallas_call | solution.py:377
  36.4 2.0 %shard_map.85 = (bf16[128,4096]{1,0:T(8,128)(2,1)}, bf16[128,4096]{1,0:T(8,128)(2,1)}, bf16[128,4096]{1,0:T(8,128)(2,1)}, bf16[128,4096]{1,0:T(8,128)(2,1)}) custom-call(bf16[128,4096]{1,0:T(8,128)(2,1)S(1)} %get-tuple-element.8.o_ref, bf16[128,4096]{1,0:T(8,128)(2,1)S(1)} %get-tuple-element.9.dq_ref, bf16[128,4096]{1,0:T(8,128)(2,1)S(1)} %get-tuple-element.10.dk_ref, ...), custom_call_target="tpu_custom_call" | custom-call | tf_op jit(solution)/shard_map/pallas_call | solution.py:424

commit v3 on v2

v3 whole, which is shorter than its diff:
```python
import functools

import jax
import jax.numpy as jnp
from jax import lax
from jax.experimental import pallas as pl
from jax.experimental.pallas import tpu as pltpu
from jax.sharding import PartitionSpec as P

SIZE = 128
F32 = jnp.float32
BF16 = jnp.bfloat16
MESH = pl.DeviceIdType.MESH


def lower_triangle(rows):
    row = lax.broadcasted_iota(jnp.int32, (rows, rows), 0)
    column = lax.broadcasted_iota(jnp.int32, (rows, rows), 1)
    return row >= column


def over_rows(left, right):
    return lax.dot_general(left, right, (((0,), (0,)), ((), ())), preferred_element_type=F32)


def over_columns(left, right):
    return lax.dot_general(left, right, (((1,), (1,)), ((), ())), preferred_element_type=F32)


def dot(left, right):
    return jnp.dot(left, right, preferred_element_type=F32)


def plan(rounds, parts):
    ready = []
    for i in range(rounds):
        ready.append((9.0 + 1.4 * i, 0.15, "sum", i))
        ready.append((14.0 + 1.4 * i, 0.35, "carry", i))
        ready.append((19.7 + 1.4 * i, 0.6, "pass", i))
        ready.append((21.1 + 1.4 * i, 0.35, "other", i))
    ready.append((8.4, 0.1, "planes", 0))
    ready.sort()
    order, now, part = [], 7.6, 0
    while ready:
        if ready[0][0] > now + 0.1 and part < parts:
            order.append(("inside", part))
            now += 8.6 / parts
            part += 1
            continue
        at, length, step, i = ready.pop(0)
        if step == "pass":
            while part < min(parts, -(-parts * (i + 1) // rounds)):
                order.append(("inside", part))
                now += 8.6 / parts
                part += 1
        order.append((step, i))
        now = max(now, at) + length
    return order


def main_kernel(
    planes, devices, q_any, k_any, v_any, g_any, d_any, out_ref,
    held, d_ref, decay_rows, forward_rows, backward_rows,
    scales, local, terms, from_core,
    to_chips, from_chips, plane_sum, from_planes, to_back, raw, states,
    own_fin, core_fin, chip_total, chip_fin, plane_fin,
    load_s, decay_s, go_s, fin_s, fin_r, chip_fs, chip_fr, plane_fs, plane_fr,
    core_s, core_r, out_s, out_r, plane_s, plane_r, back_s, back_r, last_s, last_r,
):
    heads, rows = d_any.shape
    chips = devices // 2
    own = heads // chips
    z = lax.axis_index("chain")
    me = lax.axis_index("inner")
    chip, core = me // 2, lax.rem(me, 2)
    kind = 1 - core
    ahead = core == 1

    def place(j):
        return jnp.where(ahead, j, chips - 1 - j)

    def level(j):
        return jnp.where(ahead, j, planes - 1 - j)

    depth, spot = level(z), place(chip)
    first = (depth == 0) & (spot == 0)
    last = (depth == planes - 1) & (spot == chips - 1)

    def partner(m):
        if chips & (chips - 1):
            return lax.rem(chip + m, chips)
        bits = [(1 << b, (m >> b) & 1) for b in range(chips.bit_length() - 1)]
        return sum(lax.rem(chip // size + bit, 2) * size for size, bit in bits)

    hops = sorted(range(1, chips), key=lambda m: -bin(m).count("1"))

    def at_core():
        return (z, chip * 2 + 1 - core)

    def at_chip(other):
        return (z, other * 2 + core)

    def at_plane(other):
        return (other, me)

    def remote(src, dst, send, recv, to):
        return pltpu.make_async_remote_copy(
            src_ref=src, dst_ref=dst, send_sem=send, recv_sem=recv, device_id=to, device_id_type=MESH
        )

    def columns(head):
        return pl.ds(pl.multiple_of(head * SIZE, SIZE), SIZE)

    def round_columns(i):
        return pl.ds(pl.multiple_of(i * (chips * SIZE), SIZE), chips * SIZE)

    decay_load = pltpu.make_async_copy(d_any, d_ref, decay_s)
    decay_load.start()

    @pl.loop(0, own)
    def _(i):
        taken = round_columns(i)
        for j, src in enumerate((q_any, k_any, g_any, v_any)):
            pltpu.make_async_copy(src.at[:, taken], held.at[j, :, taken], load_s.at[i]).start()

    barrier = pltpu.get_barrier_semaphore()

    def greet(to):
        pl.semaphore_signal(barrier, inc=1, device_id=to, device_id_type=MESH)

    for step in range(1, planes):
        greet((lax.rem(z + step, planes), chip * 2 + 1))
    for m in hops:
        greet((z, partner(m) * 2 + 1))
    greet(at_core())

    lower = lower_triangle(rows)
    row = lax.broadcasted_iota(jnp.int32, (rows, rows), 0)
    column = lax.broadcasted_iota(jnp.int32, (rows, rows), 1)
    upto = (row <= column).astype(F32).astype(BF16)
    after = (row > column).astype(F32).astype(BF16)
    ones = jnp.ones((rows, SIZE), BF16)
    row = lax.broadcasted_iota(jnp.int32, (heads, heads), 0)
    column = lax.broadcasted_iota(jnp.int32, (heads, heads), 1)
    owners = (column == (row % own) * chips + row // own).astype(F32).astype(BF16)

    decay_load.wait()
    decay = d_ref[...]
    decay_rows[...] = decay.astype(F32)
    by_owner = dot(dot(owners, decay).astype(BF16), ones)
    for o in range(chips):
        own_fin[o] = by_owner[o * own : (o + 1) * own]
    fin = dot(decay, ones)
    cumul = dot(decay, upto)
    forward_rows[...] = jnp.exp(cumul)
    backward_rows[...] = jnp.exp(fin - cumul)

    fin_copy = remote(own_fin, core_fin, fin_s, fin_r, at_core())

    def core_copies(begin, count, recv):
        taken = pl.ds(begin, count)
        return remote(terms.at[core, taken], from_core.at[taken], core_s, recv, at_core())

    def core_copy(i):
        return core_copies(i * chips, chips, core_r.at[i])

    @pl.when(core == 0)
    def _():
        pl.semaphore_wait(barrier, 1)
        fin_copy.start()

    def make_terms(head):
        taken = columns(head)
        keys = held[1, :, taken].T.astype(F32) * backward_rows[pl.ds(head, 1), :]
        terms[0, head] = dot(keys.astype(BF16), held[3, :, taken])
        queries = held[0, :, taken].T.astype(F32) * forward_rows[pl.ds(head, 1), :]
        terms[1, head] = dot(queries.astype(BF16), held[2, :, taken])

    @pl.loop(0, own)
    def _(i):
        part = held.at[:, :, round_columns(i)]
        pltpu.make_async_copy(part, part, load_s.at[i]).wait()
        for o in range(chips):
            make_terms(i * chips + o)

        @pl.when(core == 0)
        def _():
            core_copy(i).start()

    @pl.when(core == 1)
    def _():
        pl.semaphore_wait(barrier, 2 * (chips + planes) - 3)
        pl.semaphore_signal(go_s, inc=1, device_id=at_core(), device_id_type=MESH)
        fin_copy.start()
        for i in range(own):
            core_copy(i).start()

    @pl.when(core == 0)
    def _():
        pl.semaphore_wait(go_s, 1)

    def inside(head):
        taken = columns(head)
        query, key, grad, value = (held[j, :, taken] for j in range(4))
        picked = jnp.where(lower, decay_rows[pl.ds(head, 1), :], 0.0).astype(BF16)
        spans = dot(picked, jnp.concatenate([after, ones], axis=1))
        weights = jnp.where(lower, jnp.exp(spans[:, :rows]), 0.0)
        sums = spans[:, rows:]
        scales[0, head] = jnp.exp(sums)
        scales[1, head] = jnp.exp(own_fin[lax.rem(head, chips), pl.ds(head // chips, 1), :] - sums)
        probs = (over_columns(query, key) * weights).astype(BF16)
        grows = (over_columns(grad, value) * weights).astype(BF16)
        local[0, head] = dot(probs, value)
        local[1, head] = over_rows(probs, grad)
        local[2, head] = dot(grows, key)
        local[3, head] = over_rows(grows, query)

    def chip_fin_copy(other):
        return remote(
            chip_total.at[other], chip_fin.at[chip], chip_fs, chip_fr, at_chip(other)
        )

    def out_copy(i, other):
        to, slot = i * chips + other, i * chips + chip
        return remote(to_chips.at[to], from_chips.at[slot], out_s, out_r.at[i], at_chip(other))

    def out_copies(count, recv):
        taken = pl.ds(0, count)
        return remote(to_chips.at[taken], from_chips.at[taken], out_s, recv, at_core())

    def combine(i):
        core_copy(i).wait_recv()
        waiting = None
        for m in hops + [0]:
            other = partner(m) if m else chip
            head = i * chips + other
            factor = jnp.exp(own_fin[other, pl.ds(i, 1), :])
            total = (terms[kind, head] + factor * from_core[head]).astype(BF16)
            if m:
                to_chips[head] = total
            else:
                from_chips[head] = total
            if waiting is not None:
                @pl.when(jnp.logical_not(last))
                def _():
                    out_copy(i, waiting).start()
            waiting = other

    combine(0)
    fin_copy.wait_recv()
    chip_total[...] = own_fin[...] + core_fin[...]
    if own > 1:
        combine(1)
    chip_fin[chip] = chip_total[chip]
    for m in hops:
        chip_fin_copy(partner(m)).start()
    for i in range(2, own):
        combine(i)

    def plane_fin_copy(other):
        return remote(plane_fin.at[z], plane_fin.at[z], plane_fs, plane_fr, at_plane(other))

    def planes_step(_):
        taken = chip_fin.at[pl.ds(0, chips - 1)]
        remote(taken, taken, chip_fs, chip_fr, at_core()).wait_recv()
        total = chip_fin[0]
        for other in range(1, chips):
            total = total + chip_fin[other]
        plane_fin[z] = total
        for step in range(1, planes):
            plane_fin_copy(lax.rem(z + step, planes)).start()

    def plane_copy(i, other):
        return remote(
            plane_sum.at[i], from_planes.at[z, i], plane_s, plane_r.at[i], at_plane(other)
        )

    def factor_of(fins, at, i):
        return jnp.exp(fins[at, pl.ds(i, 1), :])

    def sum_step(i):
        fewer = (depth == planes - 1) & (spot < chips - 1)
        for few, count in ((fewer, chips - 2), (jnp.logical_not(fewer), chips - 1)):
            @pl.when(few)
            def _():
                out_copies(count, out_r.at[i]).wait_recv()

        @pl.when(depth < planes - 1)
        def _():
            total = from_chips[i * chips + place(0)].astype(F32)
            for j in range(1, chips):
                at = place(j)
                total = total * factor_of(chip_fin, at, i) + from_chips[i * chips + at].astype(F32)
            plane_sum[i] = total.astype(BF16)

            @pl.loop(0, planes - 1 - depth)
            def _(j):
                plane_copy(i, level(planes - 1 - j)).start()

    def back_copy(i, other):
        to, slot = i * chips + other, i * chips + chip
        return remote(to_back.at[to], raw.at[slot], back_s, back_r.at[i], at_chip(other))

    def back_copies(count, recv):
        taken = pl.ds(0, count)
        return remote(to_back.at[taken], raw.at[taken], back_s, recv, at_core())

    def carry_step(i):
        head = i * chips + chip
        if i == 0:
            taken = plane_fin.at[pl.ds(0, planes - 1)]
            remote(taken, taken, plane_fs, plane_fr, at_core()).wait_recv()
        for count in range(1, planes):
            @pl.when(depth == count)
            def _():
                taken = from_planes.at[pl.ds(0, count), i]
                remote(taken, taken, plane_s, plane_r.at[i], at_core()).wait_recv()

        def add_plane(j, state):
            at = level(j)
            return state * factor_of(plane_fin, at, i) + from_planes[at, i].astype(F32)

        state = lax.fori_loop(0, depth, add_plane, jnp.zeros((SIZE, SIZE), F32))
        for j in range(chips):
            at = place(j)
            to_back[i * chips + at] = state.astype(BF16)
            if j < chips - 1:
                state = state * factor_of(chip_fin, at, i) + from_chips[i * chips + at].astype(F32)
        for m in hops:
            other = partner(m)

            @pl.when((depth > 0) | (other != place(0)))
            def _():
                back_copy(i, other).start()
        raw[head] = to_back[head]

    def last_copy(i):
        taken = pl.ds(i * chips, chips)
        return remote(raw.at[taken], states.at[taken], last_s, last_r.at[i], at_core())

    def apply(which, head, state):
        taken = columns(head)
        scale = scales[which, head]
        straight = dot(held[which, :, taken], state)
        out_ref[which, :, taken] = (local[which, head] + scale * straight).astype(BF16)
        turned = over_columns(held[2 + which, :, taken], state)
        out_ref[2 + which, :, taken] = (local[2 + which, head] + scale * turned).astype(BF16)

    def pass_step(i):
        @pl.when(jnp.logical_not(first))
        def _():
            back_copies(chips - 1, back_r.at[i]).wait_recv()
        last_copy(i).start()
        for o in range(chips):
            head = i * chips + o
            factor = jnp.exp(core_fin[o, pl.ds(i, 1), :])
            apply(kind, head, (factor * raw[head].astype(F32) + from_core[head]).astype(BF16))

    def other_step(i):
        last_copy(i).wait_recv()
        for o in range(chips):
            head = i * chips + o
            apply(core, head, states[head])

    @pl.when(first)
    def _():
        @pl.loop(0, heads)
        def _(head):
            raw[head] = jnp.zeros((SIZE, SIZE), BF16)

    parts = heads // 2

    def inside_step(part):
        for j in range(2):
            inside(part * 2 + j)

    steps = {
        "planes": planes_step, "sum": sum_step, "carry": carry_step, "pass": pass_step,
        "other": other_step, "inside": inside_step,
    }
    for step, i in plan(own, parts):
        steps[step](i)

    fin_copy.wait_send()
    taken = chip_fin.at[pl.ds(0, chips - 1)]
    remote(taken, taken, chip_fs, chip_fr, at_core()).wait_send()
    taken = plane_fin.at[pl.ds(0, planes - 1)]
    remote(taken, taken, plane_fs, plane_fr, at_core()).wait_send()
    core_copies(0, heads, core_r.at[0]).wait_send()

    @pl.when(jnp.logical_not(last))
    def _():
        out_copies(own * (chips - 1), out_r.at[0]).wait_send()
    fewer = (depth == 0) & (spot > 0)
    for few, count in ((fewer, chips - 2), (jnp.logical_not(fewer), chips - 1)):
        @pl.when(few)
        def _():
            back_copies(own * count, back_r.at[0]).wait_send()
    remote(raw, states, last_s, last_r.at[0], at_core()).wait_send()
    for count in range(1, planes):
        @pl.when(planes - 1 - depth == count)
        def _():
            taken = from_planes.at[pl.ds(0, count)]
            remote(taken, taken, plane_s, plane_r.at[0], at_core()).wait_send()


def computed(planes, devices, arrays):
    decay = pltpu.with_memory_space_constraint(arrays[-1].T, pltpu.HBM)
    arrays = [pltpu.with_memory_space_constraint(item, pltpu.HBM) for item in arrays[:-1]] + [decay]
    heads, rows = decay.shape
    chips = devices // 2
    own = heads // chips
    square = (SIZE, SIZE)
    wide = arrays[0].shape
    dma = pltpu.SemaphoreType.DMA
    return pl.pallas_call(
        functools.partial(main_kernel, planes, devices),
        out_shape=jax.ShapeDtypeStruct((4,) + wide, BF16),
        in_specs=[pl.BlockSpec(memory_space=pltpu.HBM)] * 5,
        out_specs=pl.BlockSpec(memory_space=pltpu.VMEM),
        scratch_shapes=[
            pltpu.VMEM((4,) + wide, BF16),
            pltpu.VMEM((heads, rows), BF16),
            pltpu.VMEM((heads, rows), F32),
            pltpu.VMEM((heads, rows), F32),
            pltpu.VMEM((heads, rows), F32),
            pltpu.VMEM((2, heads, rows, SIZE), F32),
            pltpu.VMEM((4, heads) + square, F32),
            pltpu.VMEM((2, heads) + square, F32),
            pltpu.VMEM((heads,) + square, F32),
            pltpu.VMEM((heads,) + square, BF16),
            pltpu.VMEM((heads,) + square, BF16),
            pltpu.VMEM((own,) + square, BF16),
            pltpu.VMEM((planes, own) + square, BF16),
            pltpu.VMEM((heads,) + square, BF16),
            pltpu.VMEM((heads,) + square, BF16),
            pltpu.VMEM((heads,) + square, BF16),
            pltpu.VMEM((chips, own, SIZE), F32),
            pltpu.VMEM((chips, own, SIZE), F32),
            pltpu.VMEM((chips, own, SIZE), F32),
            pltpu.VMEM((chips, own, SIZE), F32),
            pltpu.VMEM((planes, own, SIZE), F32),
            dma((own,)), dma, pltpu.SemaphoreType.REGULAR, dma, dma, dma, dma, dma, dma,
            dma, dma((own,)), dma, dma((own,)), dma, dma((own,)),
            dma, dma((own,)), dma, dma((own,)),
        ],
        compiler_params=pltpu.CompilerParams(
            collective_id=0, has_side_effects=True, vmem_limit_bytes=48 * 2**20
        ),
    )(*arrays)


def store_kernel(held, o_out, dq_out, dk_out, dv_out, store_s):
    copies = [
        pltpu.make_async_copy(held.at[j], dst, store_s.at[j])
        for j, dst in enumerate((o_out, dv_out, dq_out, dk_out))
    ]
    for copy in copies:
        copy.start()
    for copy in copies:
        copy.wait()


def stored(results):
    return pl.pallas_call(
        store_kernel,
        out_shape=[jax.ShapeDtypeStruct(results.shape[1:], BF16)] * 4,
        in_specs=[pl.BlockSpec(memory_space=pltpu.VMEM)],
        out_specs=[pl.BlockSpec(memory_space=pltpu.HBM)] * 4,
        scratch_shapes=[pltpu.SemaphoreType.DMA((4,))],
        compiler_params=pltpu.CompilerParams(vmem_limit_bytes=2 * 2**20),
    )(results)


def solution(mesh):
    planes, devices = mesh.shape["chain"], mesh.shape["inner"]

    def shards(*arrays):
        return tuple(stored(computed(planes, devices, arrays)))

    spec = P(("chain", "inner"), None)
    return jax.shard_map(
        shards, mesh=mesh, in_specs=(spec,) * 5, out_specs=(spec,) * 4, check_vma=False
    )
```

time: 38.7 us -> 37.2 us (0.961)
  Pallas kernels: 37.8 us -> 36.3 us
    pallas_call x1, Pallas kernels: 35.8 us -> 34.3 us  [computed(): pl.pallas_call(functools.partial(main_kernel, planes, devices), out_shape...]
where the time goes in v3:
time: 37.2 us; the launch traced here: 36.9 us
  Pallas kernels  36.3 us (98%)
  between operations  0.64 us (2%)
    pallas_call x1, Pallas kernels, computed(): pl.pallas_call(functools.partial(main_kernel, planes, devices), out_shape...  34.3 us
    pallas_call x1, Pallas kernels, stored(): pl.pallas_call(store_kernel, out_shape=[jax.ShapeDtypeStruct(results.shap...  2.04 us

profile of v3, /device:TPU:0, one launch (start us, length us, event | category | flops | bytes accessed | tf_op | source)
XLA Modules:
  0.0 36.9 jit_solution(12415272279750053230)
XLA Ops:
  0.6 34.3 %shard_map.84.held = bf16[4,128,4096]{2,1,0:T(8,128)(2,1)S(1)} custom-call(bf16[128,4096]{1,0:T(8,128)(2,1)} %q_any.1, bf16[128,4096]{1,0:T(8,128)(2,1)} %k_any.1, bf16[128,4096]{1,0:T(8,128)(2,1)} %v_any.1, bf16[128,4096]{1,0:T(8,128)(2,1)} %g_any.1, bf16[32,128]{1,0:T(8,128)(2,1)} %bitcast.1), custom_call_target="tpu_custom_call" | custom-call | tf_op jit(solution)/shard_map/pallas_call | solution.py:416
  34.9 2.0 %shard_map.85 = (bf16[128,4096]{1,0:T(8,128)(2,1)}, bf16[128,4096]{1,0:T(8,128)(2,1)}, bf16[128,4096]{1,0:T(8,128)(2,1)}, bf16[128,4096]{1,0:T(8,128)(2,1)}) custom-call(bf16[4,128,4096]{2,1,0:T(8,128)(2,1)S(1)} %shard_map.84.held), custom_call_target="tpu_custom_call" | custom-call | tf_op jit(solution)/shard_map/pallas_call | solution.py:465

commit v4 on v3

--- a/solution.py
+++ b/solution.py
@@ -31,16 +31,9 @@
     return jnp.dot(left, right, preferred_element_type=F32)
 
 
-def plan(rounds, parts):
-    ready = []
-    for i in range(rounds):
-        ready.append((9.0 + 1.4 * i, 0.15, "sum", i))
-        ready.append((14.0 + 1.4 * i, 0.35, "carry", i))
-        ready.append((19.7 + 1.4 * i, 0.6, "pass", i))
-        ready.append((21.1 + 1.4 * i, 0.35, "other", i))
-    ready.append((8.4, 0.1, "planes", 0))
-    ready.sort()
-    order, now, part = [], 7.6, 0
+def plan(ready, rounds, parts, now):
+    ready = sorted(ready)
+    order, part = [], 0
     while ready:
         if ready[0][0] > now + 0.1 and part < parts:
             order.append(("inside", part))
@@ -48,7 +41,7 @@
             part += 1
             continue
         at, length, step, i = ready.pop(0)
-        if step == "pass":
+        if step in ("pass", "other"):
             while part < min(parts, -(-parts * (i + 1) // rounds)):
                 order.append(("inside", part))
                 now += 8.6 / parts
@@ -58,13 +51,36 @@
     return order
 
 
+def lead_plan(rounds, parts):
+    ready = [(7.5, 0.1, "planes", 0)]
+    for i in range(rounds):
+        ready.append((7.8 + 0.7 * i, 0.15, "sum", i))
+        ready.append((14.0 + 0.7 * i, 0.35, "carry", i))
+        ready.append((19.0 + 0.7 * i, 0.55, "pass", i))
+        ready.append((25.7 + 0.7 * i, 0.35, "other", i))
+    turn = min(2, rounds - 1)
+    ready.append((7.81 + 0.7 * turn, 0.01, "turn", 0))
+    return plan(ready, rounds, parts, 6.7)
+
+
+def tail_plan(rounds, parts):
+    ready = [(9.5, 0.1, "turn", 0), (13.3, 0.05, "share", 0)]
+    for i in range(rounds):
+        ready.append((5.1 + 0.3 * i, 0.3, "combine", i))
+        ready.append((13.4 + 0.7 * i, 0.15, "sum", i))
+        ready.append((17.5 + 0.7 * i, 0.35, "carry", i))
+        ready.append((24.6 + 0.7 * i, 0.55, "pass", i))
+        ready.append((20.1 + 0.7 * i, 0.35, "other", i))
+    return plan(ready, rounds, parts, 4.5)
+
+
 def main_kernel(
     planes, devices, q_any, k_any, v_any, g_any, d_any, out_ref,
     held, d_ref, decay_rows, forward_rows, backward_rows,
     scales, local, terms, from_core,
     to_chips, from_chips, plane_sum, from_planes, to_back, raw, states,
     own_fin, core_fin, chip_total, chip_fin, plane_fin,
-    load_s, decay_s, go_s, fin_s, fin_r, chip_fs, chip_fr, plane_fs, plane_fr,
+    load_s, decay_s, go_s, fin_s, fin_r, chip_fs, chip_fr, plane_fs, plane_fr, share_s, share_r,
     core_s, core_r, out_s, out_r, plane_s, plane_r, back_s, back_r, last_s, last_r,
 ):
     heads, rows = d_any.shape
@@ -83,6 +99,11 @@
         return jnp.where(ahead, j, planes - 1 - j)
 
     depth, spot = level(z), place(chip)
+
+    def lead_core(plane):
+        return jnp.where(plane * 2 < planes, 1, 0)
+
+    lead = core == lead_core(z)
     first = (depth == 0) & (spot == 0)
     last = (depth == planes - 1) & (spot == chips - 1)
 
@@ -129,9 +150,10 @@
         pl.semaphore_signal(barrier, inc=1, device_id=to, device_id_type=MESH)
 
     for step in range(1, planes):
-        greet((lax.rem(z + step, planes), chip * 2 + 1))
+        plane = lax.rem(z + step, planes)
+        greet((plane, chip * 2 + lead_core(plane)))
     for m in hops:
-        greet((z, partner(m) * 2 + 1))
+        greet((z, partner(m) * 2 + lead_core(z)))
     greet(at_core())
 
     lower = lower_triangle(rows)
@@ -164,11 +186,6 @@
     def core_copy(i):
         return core_copies(i * chips, chips, core_r.at[i])
 
-    @pl.when(core == 0)
-    def _():
-        pl.semaphore_wait(barrier, 1)
-        fin_copy.start()
-
     def make_terms(head):
         taken = columns(head)
         keys = held[1, :, taken].T.astype(F32) * backward_rows[pl.ds(head, 1), :]
@@ -176,28 +193,11 @@
         queries = held[0, :, taken].T.astype(F32) * forward_rows[pl.ds(head, 1), :]
         terms[1, head] = dot(queries.astype(BF16), held[2, :, taken])
 
-    @pl.loop(0, own)
-    def _(i):
+    def terms_step(i):
         part = held.at[:, :, round_columns(i)]
         pltpu.make_async_copy(part, part, load_s.at[i]).wait()
         for o in range(chips):
             make_terms(i * chips + o)
-
-        @pl.when(core == 0)
-        def _():
-            core_copy(i).start()
-
-    @pl.when(core == 1)
-    def _():
-        pl.semaphore_wait(barrier, 2 * (chips + planes) - 3)
-        pl.semaphore_signal(go_s, inc=1, device_id=at_core(), device_id_type=MESH)
-        fin_copy.start()
-        for i in range(own):
-            core_copy(i).start()
-
-    @pl.when(core == 0)
-    def _():
-        pl.semaphore_wait(go_s, 1)
 
     def inside(head):
         taken = columns(head)
@@ -228,7 +228,12 @@
         taken = pl.ds(0, count)
         return remote(to_chips.at[taken], from_chips.at[taken], out_s, recv, at_core())
 
-    def combine(i):
+    def send_out(i, other):
+        @pl.when(jnp.logical_not(last))
+        def _():
+            out_copy(i, other).start()
+
+    def combine(i, send):
         core_copy(i).wait_recv()
         waiting = None
         for m in hops + [0]:
@@ -240,25 +245,15 @@
                 to_chips[head] = total
             else:
                 from_chips[head] = total
-            if waiting is not None:
-                @pl.when(jnp.logical_not(last))
-                def _():
-                    out_copy(i, waiting).start()
+            if send and waiting is not None:
+                send_out(i, waiting)
             waiting = other
 
-    combine(0)
-    fin_copy.wait_recv()
-    chip_total[...] = own_fin[...] + core_fin[...]
-    if own > 1:
-        combine(1)
-    chip_fin[chip] = chip_total[chip]
-    for m in hops:
-        chip_fin_copy(partner(m)).start()
-    for i in range(2, own):
-        combine(i)
-
-    def plane_fin_copy(other):
-        return remote(plane_fin.at[z], plane_fin.at[z], plane_fs, plane_fr, at_plane(other))
+    def plane_fin_copy(plane, side):
+        to = (plane, chip * 2 + side)
+        return remote(plane_fin.at[z], plane_fin.at[z], plane_fs, plane_fr, to)
+
+    share_copy = remote(chip_fin, chip_fin, share_s, share_r, at_core())
 
     def planes_step(_):
         taken = chip_fin.at[pl.ds(0, chips - 1)]
@@ -267,8 +262,10 @@
         for other in range(1, chips):
             total = total + chip_fin[other]
         plane_fin[z] = total
+        share_copy.start()
         for step in range(1, planes):
-            plane_fin_copy(lax.rem(z + step, planes)).start()
+            for side in range(2):
+                plane_fin_copy(lax.rem(z + step, planes), side).start()
 
     def plane_copy(i, other):
         return remote(
@@ -374,18 +371,70 @@
         for j in range(2):
             inside(part * 2 + j)
 
+    def lead_turn(_):
+        pl.semaphore_signal(go_s, inc=1, device_id=at_core(), device_id_type=MESH)
+
+    def tail_turn(_):
+        pl.semaphore_wait(go_s, 1)
+        for i in range(own):
+            for m in hops:
+                send_out(i, partner(m))
+
     steps = {
         "planes": planes_step, "sum": sum_step, "carry": carry_step, "pass": pass_step,
         "other": other_step, "inside": inside_step,
     }
-    for step, i in plan(own, parts):
-        steps[step](i)
+
+    @pl.when(lead)
+    def _():
+        half = own // 2
+        pl.loop(0, half)(terms_step)
+        pl.semaphore_wait(barrier, 2 * (chips + planes) - 3)
+        fin_copy.start()
+        for i in range(half):
+            core_copy(i).start()
+        fin_copy.wait_recv()
+        chip_total[...] = own_fin[...] + core_fin[...]
+        chip_fin[chip] = chip_total[chip]
+        terms_step(half)
+        core_copy(half).start()
+        for m in hops:
+            chip_fin_copy(partner(m)).start()
+        combine(0, True)
+        for i in range(half + 1, own):
+            terms_step(i)
+            core_copy(i).start()
+            combine(i - half, True)
+        for i in range(own - half, own):
+            combine(i, True)
+        for step, i in lead_plan(own, parts):
+            {**steps, "turn": lead_turn}[step](i)
+        taken = chip_fin.at[pl.ds(0, chips - 1)]
+        remote(taken, taken, chip_fs, chip_fr, at_core()).wait_send()
+        share_copy.wait_send()
+        for _ in range(2):
+            taken = plane_fin.at[pl.ds(0, planes - 1)]
+            remote(taken, taken, plane_fs, plane_fr, at_core()).wait_send()
+
+    @pl.when(jnp.logical_not(lead))
+    def _():
+        pl.semaphore_wait(barrier, 1)
+        fin_copy.start()
+
+        @pl.loop(0, own)
+        def _(i):
+            terms_step(i)
+            core_copy(i).start()
+
+        fin_copy.wait_recv()
+        tail = {
+            "turn": tail_turn, "combine": lambda i: combine(i, False),
+            "share": lambda _: share_copy.wait_recv(),
+        }
+        for step, i in tail_plan(own, parts):
+            {**steps, **tail}[step](i)
 
     fin_copy.wait_send()
-    taken = chip_fin.at[pl.ds(0, chips - 1)]
-    remote(taken, taken, chip_fs, chip_fr, at_core()).wait_send()
-    taken = plane_fin.at[pl.ds(0, planes - 1)]
-    remote(taken, taken, plane_fs, plane_fr, at_core()).wait_send()
     core_copies(0, heads, core_r.at[0]).wait_send()
 
     @pl.when(jnp.logical_not(last))
@@ -440,7 +489,7 @@
             pltpu.VMEM((chips, own, SIZE), F32),
             pltpu.VMEM((chips, own, SIZE), F32),
             pltpu.VMEM((planes, own, SIZE), F32),
-            dma((own,)), dma, pltpu.SemaphoreType.REGULAR, dma, dma, dma, dma, dma, dma,
+            dma((own,)), dma, pltpu.SemaphoreType.REGULAR, dma, dma, dma, dma, dma, dma, dma, dma,
             dma, dma((own,)), dma, dma((own,)), dma, dma((own,)),
             dma, dma((own,)), dma, dma((own,)),
         ],

time: 37.2 us -> 35.5 us (0.954)
  Pallas kernels: 36.3 us -> 34.1 us
    pallas_call x1, Pallas kernels: 34.3 us -> 32 us  [computed(): pl.pallas_call(functools.partial(main_kernel, planes, devices), out_shape...]
where the time goes in v4:
time: 35.5 us; the launch traced here: 34.9 us
  Pallas kernels  34.1 us (96%)
  between operations  0.82 us (2%)
    pallas_call x1, Pallas kernels, computed(): pl.pallas_call(functools.partial(main_kernel, planes, devices), out_shape...  32 us
    pallas_call x1, Pallas kernels, stored(): pl.pallas_call(store_kernel, out_shape=[jax.ShapeDtypeStruct(results.shap...  2.04 us

profile of v4, /device:TPU:0, one launch (start us, length us, event | category | flops | bytes accessed | tf_op | source)
XLA Modules:
  0.0 34.9 jit_solution(17828561800795535188)
XLA Ops:
  0.6 32.0 %shard_map.84.held = bf16[4,128,4096]{2,1,0:T(8,128)(2,1)S(1)} custom-call(bf16[128,4096]{1,0:T(8,128)(2,1)} %q_any.1, bf16[128,4096]{1,0:T(8,128)(2,1)} %k_any.1, bf16[128,4096]{1,0:T(8,128)(2,1)} %v_any.1, bf16[128,4096]{1,0:T(8,128)(2,1)} %g_any.1, bf16[32,128]{1,0:T(8,128)(2,1)} %bitcast.1), custom_call_target="tpu_custom_call" | custom-call | tf_op jit(solution)/shard_map/pallas_call | solution.py:465
  32.7 2.0 %shard_map.85 = (bf16[128,4096]{1,0:T(8,128)(2,1)}, bf16[128,4096]{1,0:T(8,128)(2,1)}, bf16[128,4096]{1,0:T(8,128)(2,1)}, bf16[128,4096]{1,0:T(8,128)(2,1)}) custom-call(bf16[4,128,4096]{2,1,0:T(8,128)(2,1)S(1)} %shard_map.84.held), custom_call_target="tpu_custom_call" | custom-call | tf_op jit(solution)/shard_map/pallas_call | solution.py:514

commit v5 on v4

--- a/solution.py
+++ b/solution.py
@@ -11,6 +11,7 @@
 F32 = jnp.float32
 BF16 = jnp.bfloat16
 MESH = pl.DeviceIdType.MESH
+LAG = 1
 
 
 def lower_triangle(rows):
@@ -37,14 +38,14 @@
     while ready:
         if ready[0][0] > now + 0.1 and part < parts:
             order.append(("inside", part))
-            now += 8.6 / parts
+            now += 10.0 / parts
             part += 1
             continue
         at, length, step, i = ready.pop(0)
         if step in ("pass", "other"):
             while part < min(parts, -(-parts * (i + 1) // rounds)):
                 order.append(("inside", part))
-                now += 8.6 / parts
+                now += 10.0 / parts
                 part += 1
         order.append((step, i))
         now = max(now, at) + length
@@ -55,7 +56,7 @@
     ready = [(7.5, 0.1, "planes", 0)]
     for i in range(rounds):
         ready.append((7.8 + 0.7 * i, 0.15, "sum", i))
-        ready.append((14.0 + 0.7 * i, 0.35, "carry", i))
+        ready.append((13.2 + 0.7 * i, 0.35, "carry", i))
         ready.append((19.0 + 0.7 * i, 0.55, "pass", i))
         ready.append((25.7 + 0.7 * i, 0.35, "other", i))
     turn = min(2, rounds - 1)
@@ -64,7 +65,7 @@
 
 
 def tail_plan(rounds, parts):
-    ready = [(9.5, 0.1, "turn", 0), (13.3, 0.05, "share", 0)]
+    ready = [(7.9, 0.1, "turn", 0), (13.3, 0.05, "share", 0)]
     for i in range(rounds):
         ready.append((5.1 + 0.3 * i, 0.3, "combine", i))
         ready.append((13.4 + 0.7 * i, 0.15, "sum", i))
@@ -74,14 +75,26 @@
     return plan(ready, rounds, parts, 4.5)
 
 
+def late_kind(plane, planes):
+    return jnp.where(plane * 2 < planes, 1, 0)
+
+
+def apply_state(which, head, place, state, held, scales, local, out_ref):
+    taken = pl.ds(pl.multiple_of(head * SIZE, SIZE), SIZE)
+    scale = scales[which, head]
+    straight = dot(held[which, :, taken], state)
+    out_ref(0, place, (local[which, head] + scale * straight).astype(BF16))
+    turned = over_columns(held[2 + which, :, taken], state)
+    out_ref(2, place, (local[2 + which, head] + scale * turned).astype(BF16))
+
+
 def main_kernel(
-    planes, devices, q_any, k_any, v_any, g_any, d_any, out_ref,
-    held, d_ref, decay_rows, forward_rows, backward_rows,
-    scales, local, terms, from_core,
-    to_chips, from_chips, plane_sum, from_planes, to_back, raw, states,
+    planes, devices, q_any, k_any, v_any, g_any, d_any, out_ref, held, scales, local, states,
+    d_ref, decay_rows, forward_rows, backward_rows, terms, from_core,
+    to_chips, from_chips, plane_sum, from_planes, to_back, raw,
     own_fin, core_fin, chip_total, chip_fin, plane_fin,
     load_s, decay_s, go_s, fin_s, fin_r, chip_fs, chip_fr, plane_fs, plane_fr, share_s, share_r,
-    core_s, core_r, out_s, out_r, plane_s, plane_r, back_s, back_r, last_s, last_r,
+    core_s, core_r, out_s, out_r, plane_s, plane_r, back_s, back_r, late_r, last_s, last_r,
 ):
     heads, rows = d_any.shape
     chips = devices // 2
@@ -101,7 +114,7 @@
     depth, spot = level(z), place(chip)
 
     def lead_core(plane):
-        return jnp.where(plane * 2 < planes, 1, 0)
+        return late_kind(plane, planes)
 
     lead = core == lead_core(z)
     first = (depth == 0) & (spot == 0)
@@ -296,13 +309,25 @@
 
     def back_copy(i, other):
         to, slot = i * chips + other, i * chips + chip
-        return remote(to_back.at[to], raw.at[slot], back_s, back_r.at[i], at_chip(other))
+        recv = back_r.at[i] if i < own - 1 else late_r.at[chip]
+        return remote(to_back.at[to], raw.at[slot], back_s, recv, at_chip(other))
 
     def back_copies(count, recv):
         taken = pl.ds(0, count)
         return remote(to_back.at[taken], raw.at[taken], back_s, recv, at_core())
 
-    def carry_step(i):
+    def send_back(i, to_first):
+        for m in hops:
+            other = partner(m)
+            wanted = (depth > 0) | (other != place(0))
+            if to_first is not None:
+                wanted = wanted & ((other == 0) if to_first else (other != 0))
+
+            @pl.when(wanted)
+            def _():
+                back_copy(i, other).start()
+
+    def carry_step(i, lag=0):
         head = i * chips + chip
         if i == 0:
             taken = plane_fin.at[pl.ds(0, planes - 1)]
@@ -323,38 +348,59 @@
             to_back[i * chips + at] = state.astype(BF16)
             if j < chips - 1:
                 state = state * factor_of(chip_fin, at, i) + from_chips[i * chips + at].astype(F32)
-        for m in hops:
-            other = partner(m)
-
-            @pl.when((depth > 0) | (other != place(0)))
-            def _():
-                back_copy(i, other).start()
+        if lag == 0:
+            send_back(i, None)
+        else:
+            send_back(i, True)
+            if i >= lag:
+                send_back(i - lag, False)
+            if i == own - 1:
+                for late in range(max(own - lag, 0), own):
+                    send_back(late, False)
         raw[head] = to_back[head]
+
+    def last_part(i, other):
+        head = i * chips + other
+        return remote(raw.at[head], states.at[head], last_s, last_r.at[i], at_core())
 
     def last_copy(i):
         taken = pl.ds(i * chips, chips)
         return remote(raw.at[taken], states.at[taken], last_s, last_r.at[i], at_core())
 
     def apply(which, head, state):
-        taken = columns(head)
-        scale = scales[which, head]
-        straight = dot(held[which, :, taken], state)
-        out_ref[which, :, taken] = (local[which, head] + scale * straight).astype(BF16)
-        turned = over_columns(held[2 + which, :, taken], state)
-        out_ref[2 + which, :, taken] = (local[2 + which, head] + scale * turned).astype(BF16)
-
-    def pass_step(i):
-        @pl.when(jnp.logical_not(first))
-        def _():
-            back_copies(chips - 1, back_r.at[i]).wait_recv()
-        last_copy(i).start()
+        def put(j, taken, value):
+            out_ref[j + which, :, taken] = value
+
+        apply_state(which, head, columns(head), state, held, scales, local, put)
+
+    def pass_step(i, late):
+        if i < own - 1:
+            @pl.when(jnp.logical_not(first))
+            def _():
+                back_copies(chips - 1, back_r.at[i]).wait_recv()
+            last_copy(i).start()
+        else:
+            last_part(i, chip).start()
+            for m in hops:
+                other = partner(m)
+
+                @pl.when(jnp.logical_not(first))
+                def _():
+                    back_copies(1, late_r.at[other]).wait_recv()
+                last_part(i, other).start()
         for o in range(chips):
             head = i * chips + o
             factor = jnp.exp(core_fin[o, pl.ds(i, 1), :])
-            apply(kind, head, (factor * raw[head].astype(F32) + from_core[head]).astype(BF16))
-
-    def other_step(i):
+            state = (factor * raw[head].astype(F32) + from_core[head]).astype(BF16)
+            if late and i == own - 1:
+                states[head] = state
+            else:
+                apply(kind, head, state)
+
+    def other_step(i, late):
         last_copy(i).wait_recv()
+        if late and i == own - 1:
+            return
         for o in range(chips):
             head = i * chips + o
             apply(core, head, states[head])
@@ -381,8 +427,7 @@
                 send_out(i, partner(m))
 
     steps = {
-        "planes": planes_step, "sum": sum_step, "carry": carry_step, "pass": pass_step,
-        "other": other_step, "inside": inside_step,
+        "planes": planes_step, "sum": sum_step, "carry": carry_step, "inside": inside_step,
     }
 
     @pl.when(lead)
@@ -407,8 +452,12 @@
             combine(i - half, True)
         for i in range(own - half, own):
             combine(i, True)
+        front = {
+            "turn": lead_turn, "pass": lambda i: pass_step(i, False),
+            "other": lambda i: other_step(i, True),
+        }
         for step, i in lead_plan(own, parts):
-            {**steps, "turn": lead_turn}[step](i)
+            {**steps, **front}[step](i)
         taken = chip_fin.at[pl.ds(0, chips - 1)]
         remote(taken, taken, chip_fs, chip_fr, at_core()).wait_send()
         share_copy.wait_send()
@@ -429,7 +478,8 @@
         fin_copy.wait_recv()
         tail = {
             "turn": tail_turn, "combine": lambda i: combine(i, False),
-            "share": lambda _: share_copy.wait_recv(),
+            "share": lambda _: share_copy.wait_recv(), "carry": lambda i: carry_step(i, LAG),
+            "pass": lambda i: pass_step(i, True), "other": lambda i: other_step(i, False),
         }
         for step, i in tail_plan(own, parts):
             {**steps, **tail}[step](i)
@@ -464,24 +514,26 @@
     dma = pltpu.SemaphoreType.DMA
     return pl.pallas_call(
         functools.partial(main_kernel, planes, devices),
-        out_shape=jax.ShapeDtypeStruct((4,) + wide, BF16),
+        out_shape=[
+            jax.ShapeDtypeStruct((4,) + wide, BF16),
+            jax.ShapeDtypeStruct((4,) + wide, BF16),
+            jax.ShapeDtypeStruct((2, heads, rows, SIZE), F32),
+            jax.ShapeDtypeStruct((4, heads) + square, F32),
+            jax.ShapeDtypeStruct((heads,) + square, BF16),
+        ],
         in_specs=[pl.BlockSpec(memory_space=pltpu.HBM)] * 5,
-        out_specs=pl.BlockSpec(memory_space=pltpu.VMEM),
+        out_specs=[pl.BlockSpec(memory_space=pltpu.VMEM)] * 5,
         scratch_shapes=[
-            pltpu.VMEM((4,) + wide, BF16),
             pltpu.VMEM((heads, rows), BF16),
             pltpu.VMEM((heads, rows), F32),
             pltpu.VMEM((heads, rows), F32),
             pltpu.VMEM((heads, rows), F32),
-            pltpu.VMEM((2, heads, rows, SIZE), F32),
-            pltpu.VMEM((4, heads) + square, F32),
             pltpu.VMEM((2, heads) + square, F32),
             pltpu.VMEM((heads,) + square, F32),
             pltpu.VMEM((heads,) + square, BF16),
             pltpu.VMEM((heads,) + square, BF16),
             pltpu.VMEM((own,) + square, BF16),
             pltpu.VMEM((planes, own) + square, BF16),
-            pltpu.VMEM((heads,) + square, BF16),
             pltpu.VMEM((heads,) + square, BF16),
             pltpu.VMEM((heads,) + square, BF16),
             pltpu.VMEM((chips, own, SIZE), F32),
@@ -491,41 +543,78 @@
             pltpu.VMEM((planes, own, SIZE), F32),
             dma((own,)), dma, pltpu.SemaphoreType.REGULAR, dma, dma, dma, dma, dma, dma, dma, dma,
             dma, dma((own,)), dma, dma((own,)), dma, dma((own,)),
-            dma, dma((own,)), dma, dma((own,)),
+            dma, dma((own,)), dma((chips,)), dma, dma((own,)),
         ],
         compiler_params=pltpu.CompilerParams(
-            collective_id=0, has_side_effects=True, vmem_limit_bytes=48 * 2**20
+            collective_id=0, has_side_effects=True, vmem_limit_bytes=20 * 2**20
         ),
     )(*arrays)
 
 
-def store_kernel(held, o_out, dq_out, dk_out, dv_out, store_s):
+def store_kernel(
+    planes, chips, done, held, scales, local, states, o_out, dq_out, dk_out, dv_out, fresh, store_s, late_s
+):
+    heads = states.shape[0]
+    width = chips * SIZE
+    split = heads * SIZE - width
+    which = late_kind(lax.axis_index("chain"), planes)
+    outs = (o_out, dv_out, dq_out, dk_out)
+    early, late = pl.ds(0, split), pl.ds(split, width)
     copies = [
-        pltpu.make_async_copy(held.at[j], dst, store_s.at[j])
-        for j, dst in enumerate((o_out, dv_out, dq_out, dk_out))
+        pltpu.make_async_copy(done.at[j, :, early], dst.at[:, early], store_s.at[j])
+        for j, dst in enumerate(outs)
     ]
     for copy in copies:
         copy.start()
+
+    def late_copies(kind):
+        pairs = []
+        for j in range(2):
+            pairs.append((fresh.at[j], outs[2 * j + kind]))
+            pairs.append((done.at[2 * j + 1 - kind, :, late], outs[2 * j + 1 - kind]))
+        return [
+            pltpu.make_async_copy(src, dst.at[:, late], late_s.at[j])
+            for j, (src, dst) in enumerate(pairs)
+        ]
+
+    def put(j, taken, value):
+        fresh[j // 2, :, taken] = value
+
+    for o in range(chips):
+        head = heads - chips + o
+        apply_state(which, head, pl.ds(o * SIZE, SIZE), states[head], held, scales, local, put)
+    for kind in range(2):
+        @pl.when(which == kind)
+        def _():
+            for copy in late_copies(kind):
+                copy.start()
+            for copy in late_copies(kind):
+                copy.wait()
     for copy in copies:
         copy.wait()
 
 
-def stored(results):
+def stored(planes, chips, results):
+    rows, features = results[0].shape[1:]
     return pl.pallas_call(
-        store_kernel,
-        out_shape=[jax.ShapeDtypeStruct(results.shape[1:], BF16)] * 4,
-        in_specs=[pl.BlockSpec(memory_space=pltpu.VMEM)],
+        functools.partial(store_kernel, planes, chips),
+        out_shape=[jax.ShapeDtypeStruct((rows, features), BF16)] * 4,
+        in_specs=[pl.BlockSpec(memory_space=pltpu.VMEM)] * 5,
         out_specs=[pl.BlockSpec(memory_space=pltpu.HBM)] * 4,
-        scratch_shapes=[pltpu.SemaphoreType.DMA((4,))],
-        compiler_params=pltpu.CompilerParams(vmem_limit_bytes=2 * 2**20),
-    )(results)
+        scratch_shapes=[
+            pltpu.VMEM((2, rows, chips * SIZE), BF16),
+            pltpu.SemaphoreType.DMA((4,)),
+            pltpu.SemaphoreType.DMA((4,)),
+        ],
+        compiler_params=pltpu.CompilerParams(vmem_limit_bytes=4 * 2**20),
+    )(*results)
 
 
 def solution(mesh):
     planes, devices = mesh.shape["chain"], mesh.shape["inner"]
 
     def shards(*arrays):
-        return tuple(stored(computed(planes, devices, arrays)))
+        return tuple(stored(planes, devices // 2, computed(planes, devices, arrays)))
 
     spec = P(("chain", "inner"), None)
     return jax.shard_map(

time: 35.5 us -> 34.5 us (0.972)
  the two profiles are of different devices: /device:TPU:0 before, /device:TPU:3 now
where the time goes in v5:
time: 34.5 us; the launch traced here: 34.3 us
  Pallas kernels  33.4 us (97%)
  between operations  0.82 us (2%)
    pallas_call x1, Pallas kernels, computed(): pl.pallas_call(functools.partial(main_kernel, planes, devices), out_shape...  31.3 us
    pallas_call x1, Pallas kernels, stored(): pl.pallas_call(functools.partial(store_kernel, planes, chips), out_shape=...  2.13 us

profile of v5, /device:TPU:3, one launch (start us, length us, event | category | flops | bytes accessed | tf_op | source)
XLA Modules:
  0.0 34.3 jit_solution(4509054290616352189)
XLA Ops:
  0.6 31.3 %shard_map.84 = (bf16[4,128,4096]{2,1,0:T(8,128)(2,1)S(1)}, bf16[4,128,4096]{2,1,0:T(8,128)(2,1)S(1)}, f32[2,32,128,128]{3,2,1,0:T(8,128)S(1)}, f32[4,32,128,128]{3,2,1,0:T(8,128)S(1)}, bf16[32,128,128]{2,1,0:T(8,128)(2,1)S(1)}) custom-call(bf16[128,4096]{1,0:T(8,128)(2,1)} %q_any.1, bf16[128,4096]{1,0:T(8,128)(2,1)} %k_any.1, bf16[128,4096]{1,0:T(8,128)(2,1)} %v_any.1, ...), custom_call_target="tpu_custom_call" | custom-call | tf_op jit(solution)/shard_map/pallas_call | solution.py:515
  31.9 2.1 %shard_map.85 = (bf16[128,4096]{1,0:T(8,128)(2,1)}, bf16[128,4096]{1,0:T(8,128)(2,1)}, bf16[128,4096]{1,0:T(8,128)(2,1)}, bf16[128,4096]{1,0:T(8,128)(2,1)}) custom-call(bf16[4,128,4096]{2,1,0:T(8,128)(2,1)S(1)} %get-tuple-element.9.done, bf16[4,128,4096]{2,1,0:T(8,128)(2,1)S(1)} %get-tuple-element.10.held, ...), custom_call_target="tpu_custom_call" | custom-call | tf_op jit(solution)/shard_map/pallas_call | solution.py:599

commit v6 on v5

--- a/solution.py
+++ b/solution.py
@@ -94,7 +94,7 @@
     to_chips, from_chips, plane_sum, from_planes, to_back, raw,
     own_fin, core_fin, chip_total, chip_fin, plane_fin,
     load_s, decay_s, go_s, fin_s, fin_r, chip_fs, chip_fr, plane_fs, plane_fr, share_s, share_r,
-    core_s, core_r, out_s, out_r, plane_s, plane_r, back_s, back_r, late_r, last_s, last_r,
+    core_s, core_r, out_s, out_r, plane_s, plane_r, back_s, back_r, late_r, last_s,
 ):
     heads, rows = d_any.shape
     chips = devices // 2
@@ -126,7 +126,7 @@
         bits = [(1 << b, (m >> b) & 1) for b in range(chips.bit_length() - 1)]
         return sum(lax.rem(chip // size + bit, 2) * size for size, bit in bits)
 
-    hops = sorted(range(1, chips), key=lambda m: -bin(m).count("1"))
+    hops = range(chips - 1, 0, -1)
 
     def at_core():
         return (z, chip * 2 + 1 - core)
@@ -249,7 +249,7 @@
     def combine(i, send):
         core_copy(i).wait_recv()
         waiting = None
-        for m in hops + [0]:
+        for m in [*hops, 0]:
             other = partner(m) if m else chip
             head = i * chips + other
             factor = jnp.exp(own_fin[other, pl.ds(i, 1), :])
@@ -361,11 +361,11 @@
 
     def last_part(i, other):
         head = i * chips + other
-        return remote(raw.at[head], states.at[head], last_s, last_r.at[i], at_core())
+        return remote(raw.at[head], states.at[head], last_s, load_s.at[i], at_core())
 
     def last_copy(i):
         taken = pl.ds(i * chips, chips)
-        return remote(raw.at[taken], states.at[taken], last_s, last_r.at[i], at_core())
+        return remote(raw.at[taken], states.at[taken], last_s, load_s.at[i], at_core())
 
     def apply(which, head, state):
         def put(j, taken, value):
@@ -495,7 +495,7 @@
         @pl.when(few)
         def _():
             back_copies(own * count, back_r.at[0]).wait_send()
-    remote(raw, states, last_s, last_r.at[0], at_core()).wait_send()
+    remote(raw, states, last_s, load_s.at[0], at_core()).wait_send()
     for count in range(1, planes):
         @pl.when(planes - 1 - depth == count)
         def _():
@@ -543,7 +543,7 @@
             pltpu.VMEM((planes, own, SIZE), F32),
             dma((own,)), dma, pltpu.SemaphoreType.REGULAR, dma, dma, dma, dma, dma, dma, dma, dma,
             dma, dma((own,)), dma, dma((own,)), dma, dma((own,)),
-            dma, dma((own,)), dma((chips,)), dma, dma((own,)),
+            dma, dma((own,)), dma((chips,)), dma,
         ],
         compiler_params=pltpu.CompilerParams(
             collective_id=0, has_side_effects=True, vmem_limit_bytes=20 * 2**20
@@ -552,7 +552,7 @@
 
 
 def store_kernel(
-    planes, chips, done, held, scales, local, states, o_out, dq_out, dk_out, dv_out, fresh, store_s, late_s
+    planes, chips, done, held, scales, local, states, o_out, dq_out, dk_out, dv_out, fresh, store_s
 ):
     heads = states.shape[0]
     width = chips * SIZE
@@ -561,7 +561,7 @@
     outs = (o_out, dv_out, dq_out, dk_out)
     early, late = pl.ds(0, split), pl.ds(split, width)
     copies = [
-        pltpu.make_async_copy(done.at[j, :, early], dst.at[:, early], store_s.at[j])
+        pltpu.make_async_copy(done.at[j, :, early], dst.at[:, early], store_s)
         for j, dst in enumerate(outs)
     ]
     for copy in copies:
@@ -573,8 +573,8 @@
             pairs.append((fresh.at[j], outs[2 * j + kind]))
             pairs.append((done.at[2 * j + 1 - kind, :, late], outs[2 * j + 1 - kind]))
         return [
-            pltpu.make_async_copy(src, dst.at[:, late], late_s.at[j])
-            for j, (src, dst) in enumerate(pairs)
+            pltpu.make_async_copy(src, dst.at[:, late], store_s)
+            for src, dst in pairs
         ]
 
     def put(j, taken, value):
@@ -588,10 +588,7 @@
         def _():
             for copy in late_copies(kind):
                 copy.start()
-            for copy in late_copies(kind):
-                copy.wait()
-    for copy in copies:
-        copy.wait()
+    pltpu.make_async_copy(done, done, store_s).wait()
 
 
 def stored(planes, chips, results):
@@ -603,8 +600,7 @@
         out_specs=[pl.BlockSpec(memory_space=pltpu.HBM)] * 4,
         scratch_shapes=[
             pltpu.VMEM((2, rows, chips * SIZE), BF16),
-            pltpu.SemaphoreType.DMA((4,)),
-            pltpu.SemaphoreType.DMA((4,)),
+            pltpu.SemaphoreType.DMA,
         ],
         compiler_params=pltpu.CompilerParams(vmem_limit_bytes=4 * 2**20),
     )(*results)

time: 34.5 us -> 34.4 us (level)
  no operation moved by 1% of the time
where the time goes in v6:
time: 34.4 us; the launch traced here: 34.2 us
  Pallas kernels  33.3 us (97%)
  between operations  0.82 us (2%)
    pallas_call x1, Pallas kernels, computed(): pl.pallas_call(functools.partial(main_kernel, planes, devices), out_shape...  31.3 us
    pallas_call x1, Pallas kernels, stored(): pl.pallas_call(functools.partial(store_kernel, planes, chips), out_shape=...  2.07 us

profile of v6, /device:TPU:3, one launch (start us, length us, event | category | flops | bytes accessed | tf_op | source)
XLA Modules:
  0.0 34.2 jit_solution(13513157754077091830)
XLA Ops:
  0.6 31.3 %shard_map.84 = (bf16[4,128,4096]{2,1,0:T(8,128)(2,1)S(1)}, bf16[4,128,4096]{2,1,0:T(8,128)(2,1)S(1)}, f32[2,32,128,128]{3,2,1,0:T(8,128)S(1)}, f32[4,32,128,128]{3,2,1,0:T(8,128)S(1)}, bf16[32,128,128]{2,1,0:T(8,128)(2,1)S(1)}) custom-call(bf16[128,4096]{1,0:T(8,128)(2,1)} %q_any.1, bf16[128,4096]{1,0:T(8,128)(2,1)} %k_any.1, bf16[128,4096]{1,0:T(8,128)(2,1)} %v_any.1, ...), custom_call_target="tpu_custom_call" | custom-call | tf_op jit(solution)/shard_map/pallas_call | solution.py:515
  31.9 2.1 %shard_map.85 = (bf16[128,4096]{1,0:T(8,128)(2,1)}, bf16[128,4096]{1,0:T(8,128)(2,1)}, bf16[128,4096]{1,0:T(8,128)(2,1)}, bf16[128,4096]{1,0:T(8,128)(2,1)}) custom-call(bf16[4,128,4096]{2,1,0:T(8,128)(2,1)S(1)} %get-tuple-element.9.done, bf16[4,128,4096]{2,1,0:T(8,128)(2,1)S(1)} %get-tuple-element.10.held, ...), custom_call_target="tpu_custom_call" | custom-call | tf_op jit(solution)/shard_map/pallas_call | solution.py:596

commit v7 on v6

--- a/solution.py
+++ b/solution.py
@@ -71,7 +71,7 @@
         ready.append((13.4 + 0.7 * i, 0.15, "sum", i))
         ready.append((17.5 + 0.7 * i, 0.35, "carry", i))
         ready.append((24.6 + 0.7 * i, 0.55, "pass", i))
-        ready.append((20.1 + 0.7 * i, 0.35, "other", i))
+        ready.append((21.4 + 0.7 * i, 0.35, "other", i))
     return plan(ready, rounds, parts, 4.5)
 
 

time: 34.4 us -> 34.1 us (level)
  no operation moved by 1% of the time
where the time goes in v7:
time: 34.1 us; the launch traced here: 33.9 us
  Pallas kernels  33.1 us (97%)
  between operations  0.82 us (2%)
    pallas_call x1, Pallas kernels, computed(): pl.pallas_call(functools.partial(main_kernel, planes, devices), out_shape...  31 us
    pallas_call x1, Pallas kernels, stored(): pl.pallas_call(functools.partial(store_kernel, planes, chips), out_shape=...  2.06 us

profile of v7, /device:TPU:3, one launch (start us, length us, event | category | flops | bytes accessed | tf_op | source)
XLA Modules:
  0.0 33.9 jit_solution(6681581998128290899)
XLA Ops:
  0.6 31.0 %shard_map.84 = (bf16[4,128,4096]{2,1,0:T(8,128)(2,1)S(1)}, bf16[4,128,4096]{2,1,0:T(8,128)(2,1)S(1)}, f32[2,32,128,128]{3,2,1,0:T(8,128)S(1)}, f32[4,32,128,128]{3,2,1,0:T(8,128)S(1)}, bf16[32,128,128]{2,1,0:T(8,128)(2,1)S(1)}) custom-call(bf16[128,4096]{1,0:T(8,128)(2,1)} %q_any.1, bf16[128,4096]{1,0:T(8,128)(2,1)} %k_any.1, bf16[128,4096]{1,0:T(8,128)(2,1)} %v_any.1, ...), custom_call_target="tpu_custom_call" | custom-call | tf_op jit(solution)/shard_map/pallas_call | solution.py:515
  31.6 2.1 %shard_map.85 = (bf16[128,4096]{1,0:T(8,128)(2,1)}, bf16[128,4096]{1,0:T(8,128)(2,1)}, bf16[128,4096]{1,0:T(8,128)(2,1)}, bf16[128,4096]{1,0:T(8,128)(2,1)}) custom-call(bf16[4,128,4096]{2,1,0:T(8,128)(2,1)S(1)} %get-tuple-element.9.done, bf16[4,128,4096]{2,1,0:T(8,128)(2,1)S(1)} %get-tuple-element.10.held, ...), custom_call_target="tpu_custom_call" | custom-call | tf_op jit(solution)/shard_map/pallas_call | solution.py:596
